TPU v7x, 256 devices: a whole 4x4x8 slice. The times are simulated.
256 devices in a mesh: gx: 16 (over z_lo, x), gy: 4 (over y), gz: 4 (over z_hi, core).
Axes of the slice: x: 4, y: 4, z: 8 (z_hi: 2, z_lo: 4; z = z_hi * 4 + z_lo), core: 2. Of those that a mesh axis runs over, the one named last changes fastest.
Arguments:
- tokens: bfloat16 [8192, 4608], P('gx', 'gy'), may hold values from -6 to 6
- base_up_weight: bfloat16 [4608, 18432], P('gy', ('gz', 'gx')), may hold values from -0.09375 to 0.09375
- adapter_down_weight: bfloat16 [64, 16, 4608], P(None, None, 'gy'), may hold values from -0.09375 to 0.09375
- adapter_up_weight: bfloat16 [64, 16, 18432], P('gx', None, 'gz'), may hold values from -1.5 to 1.5
- block_adapter_index: int32 [64], P('gx'), may hold values from 0 to 63
- request_rows: int32 [64], P('gx'), may hold values from 1 to 128
Outputs:
- projected: bfloat16 [8192, 18432], P(('gx', 'gy'), 'gz')
Inputs may be any that keep to these rules, and one draw needn't show every extreme that they name: `request_rows`: live rows of each block.
All inputs are finite; a program needn't handle non-finite values.
Results may differ from a plain program's by a relative error of at most 0.0047.
Values may be sent and summed in bfloat16 or wider, within the bound.
A program may use at most 128 MiB of HBM per device.

v0:
```python
import jax
import jax.numpy as jnp
from jax import lax
from jax.sharding import PartitionSpec as P

ADAPTER_COUNT = 64
BLOCK = 128


def sent_to_all(array, axis):
    size = lax.axis_size(axis)
    return lax.all_to_all(
        jnp.broadcast_to(array[None], (size, *array.shape)), axis, 0, 0, tiled=True
    )


def taken_together(array, axis):
    return sent_to_all(array, axis).sum(axis=0)


def in_blocks(array, dim, size):
    before, after = (array.shape[:dim], array.shape[dim + 1 :])
    return jnp.moveaxis(array.reshape(*before, size, -1, *after), dim, 0)


def summed_on_arrival(array, axis, dim):
    size = lax.axis_size(axis)
    tiles = lax.all_to_all(in_blocks(array, dim, size), axis, 0, 0, tiled=True)
    return jnp.sum(tiles.astype(jnp.float32), axis=0)


def body(
    tokens,
    base_up_weight,
    adapter_down_weight,
    adapter_up_weight,
    block_adapter_index,
    request_rows,
):
    rows, shard_width = tokens.shape
    groups = lax.axis_size("gy")
    blocks = rows // BLOCK
    own_blocks = blocks // groups
    own_rows = own_blocks * BLOCK
    first = lax.axis_index("gy") * own_blocks
    rank_values = adapter_down_weight.shape[1]
    catalog = jnp.arange(ADAPTER_COUNT, dtype=jnp.int32)
    selected_adapters = (block_adapter_index[:, None] == catalog[None, :]).astype(jnp.bfloat16)
    chosen_down = jnp.dot(
        selected_adapters,
        adapter_down_weight.reshape(ADAPTER_COUNT, rank_values * shard_width),
        preferred_element_type=jnp.float32,
    )
    chosen_down = chosen_down.astype(jnp.bfloat16).reshape(blocks, rank_values, shard_width)
    tok_blocks = tokens.reshape(blocks, BLOCK, shard_width)
    shrink_part = jnp.einsum(
        "bmd,brd->bmr", tok_blocks, chosen_down, preferred_element_type=jnp.float32
    )
    shrink_all = taken_together(shrink_part, "gy")
    shrink_own = lax.dynamic_slice_in_dim(shrink_all, first, own_blocks, 0)
    shrink_low = shrink_own.astype(jnp.bfloat16)
    adapter_factors = lax.all_gather(adapter_up_weight, "gx", axis=0, tiled=True)
    out_width = adapter_factors.shape[2]
    own_picks = lax.dynamic_slice_in_dim(selected_adapters, first, own_blocks, 0)
    chosen_up = jnp.dot(
        own_picks,
        adapter_factors.reshape(ADAPTER_COUNT, rank_values * out_width),
        preferred_element_type=jnp.float32,
    )
    chosen_up = chosen_up.astype(jnp.bfloat16).reshape(own_blocks, rank_values, out_width)
    expand = jnp.einsum("bmr,brf->bmf", shrink_low, chosen_up, preferred_element_type=jnp.float32)
    expand = expand.reshape(own_rows, out_width)
    partial_value = jnp.dot(
        tokens,
        lax.all_gather(base_up_weight, "gx", axis=1, tiled=True),
        preferred_element_type=jnp.float32,
    )
    extra = 2.0 * expand
    total = summed_on_arrival(partial_value.astype(jnp.bfloat16), "gy", 0) + extra
    own_live = lax.dynamic_slice_in_dim(request_rows, first, own_blocks, 0)
    live_mask = (jnp.arange(BLOCK, dtype=jnp.int32)[None, :] < own_live[:, None]).reshape(
        own_rows, 1
    )
    return jnp.where(live_mask, total, 0.0).astype(jnp.bfloat16)


def solution(mesh):
    in_specs = (
        P("gx", "gy"),
        P("gy", ("gz", "gx")),
        P(None, None, "gy"),
        P("gx", None, "gz"),
        P("gx"),
        P("gx"),
    )
    out_specs = P(("gx", "gy"), "gz")
    return jax.shard_map(body, mesh=mesh, in_specs=in_specs, out_specs=out_specs, check_vma=False)
```

profile of v0, /device:TPU:8, one launch (start us, length us, event | category | flops | bytes accessed | tf_op | source)
XLA Modules:
  0.0 278.0 jit_solution(411881308684127946)
XLA Ops:
  6.5 0.0 copy-start
  6.5 0.0 all-gather.3.cloned.1.call-start
  6.5 0.7 all-gather.3.cloned.1.call-update
  7.3 0.0 all-gather.5.cloned.1.call-start
  7.3 0.7 all-gather.5.cloned.1.call-update
  8.0 2.2 copy.8
  10.2 0.5 convolution_convert_fusion
  10.7 0.4 convolution_bitcast_fusion
  11.2 0.7 broadcast_in_dim.11
  11.8 5.4 %all-to-all-start.1 = ((f32[4,4,128,16]{2,3,1,0:T(8,128)}), f32[4,4,128,16]{2,3,1,0:T(8,128)S(1)}, u32[]{:S(2)}, u32[]{:S(2)}) async-start(f32[4,4,128,16]{2,3,1,0:T(8,128)} %broadcast_in_dim.11), calls=%async_computation.1 | async-start | bytes 262144 | tf_op jit(solution)/shard_map/all_to_all | solution.py:12
  17.3 119.5 %all-gather.3.cloned.1.call-done = bf16[1152,4608]{0,1:T(8,128)(2,1)} async-done(((bf16[1152,288]{0,1:T(8,128)(2,1)}), bf16[1152,4608]{0,1:T(8,128)(2,1)}) %all-gather.3.cloned.1.call-update) | async-done | bytes 10616848 | tf_op jit(solution)/shard_map/all_gather | solution.py:75
  136.8 11.9 %convolution_convert_fusion.1 = bf16[512,4608]{1,0:T(8,128)(2,1)} fusion(bf16[512,1152]{1,0:T(8,128)(2,1)S(1)} %copy-done, bf16[1152,4608]{0,1:T(8,128)(2,1)} %all-gather.3.cloned.1.call-done), kind=kOutput, calls=%fused_computation.2 | convolution fusion | flops 5438177280 | bytes 16515072 | tf_op jit(solution)/shard_map/dot_general | solution.py:73
  148.7 0.0 all-to-all-done.1
  148.7 5.6 %all-to-all-start = ((bf16[4,128,4608]{2,1,0:T(8,128)(2,1)}), bf16[4,128,4608]{2,1,0:T(8,128)(2,1)}, u32[]{:S(2)}, u32[]{:S(2)}) async-start(bf16[4,128,4608]{2,1,0:T(8,128)(2,1)} %bitcast.31), calls=%async_computation | async-start | bytes 9437184 | tf_op jit(solution)/shard_map/all_to_all | solution.py:28
  154.3 0.6 dynamic_slice.9
  154.9 0.6 iota_compare_fusion.1
  155.5 0.1 iota_compare_fusion
  155.6 92.7 %all-gather.5.cloned.1.call-done = bf16[64,16,4608]{2,1,0:T(8,128)(2,1)} async-done(((bf16[4,16,4608]{2,1,0:T(8,128)(2,1)}), bf16[64,16,4608]{2,1,0:T(8,128)(2,1)}) %all-gather.5.cloned.1.call-update) | async-done | bytes 9437200 | tf_op jit(solution)/shard_map/all_gather | solution.py:62
  248.3 12.8 %copy.10 = bf16[8,8,16,4608]{3,1,2,0:T(8,128)(2,1)} copy(bf16[8,8,16,4608]{3,2,1,0:T(8,128)(2,1)} %bitcast.29) | data formatting | bytes 18874368
  261.1 5.1 %fusion.7 = f32[1,73728]{1,0:T(1,128)S(1)} fusion(bf16[64,73728]{1,0:T(8,128)(2,1)} %bitcast.28, pred[4,64]{1,0:T(4,128)(4,1)S(1)} %iota_compare_fusion, s32[]{:T(128)S(6)} %select_n.9), kind=kOutput, calls=%fused_computation.13 | convolution fusion | flops 9437184 | bytes 9732356 | tf_op jit(solution)/shard_map/dot_general | solution.py:65
  266.2 0.2 reshape.51
  266.3 0.0 all-to-all-done
  266.4 3.3 %convert_reduce_fusion = f32[128,4608]{1,0:T(8,128)S(1)} fusion(bf16[4,128,4608]{2,1,0:T(8,128)(2,1)} %all-to-all-done), kind=kLoop, calls=%fused_computation.1 | loop fusion | flops 4128768 | bytes 7077888 | tf_op jit(solution)/shard_map/reduce_sum | solution.py:29
  269.7 1.5 fusion.2
  (7 shorter events, 0.0 us)
Async XLA Ops:
  6.5 4.2 %copy-start = (bf16[512,1152]{1,0:T(8,128)(2,1)S(1)}, bf16[512,1152]{1,0:T(8,128)(2,1)}, u32[]{:S(2)}) copy-start(bf16[512,1152]{1,0:T(8,128)(2,1)} %param.6) | copy-start | bytes 3538948
  6.5 130.2 %all-gather.3.cloned.1.call-start = ((), (), s32[]{:S(2)}) async-start(), calls=%async_computation.2 | async-start | bytes 11280384 | tf_op jit(solution)/shard_map/all_gather | solution.py:75
  7.3 241.0 %all-gather.5.cloned.1.call-start = ((), (), s32[]{:S(2)}) async-start(), calls=%async_computation.3 | async-start | bytes 10027008 | tf_op jit(solution)/shard_map/all_gather | solution.py:62
  8.0 2.2 copy-start.1
  11.8 136.9 %all-to-all-start.1 = ((f32[4,4,128,16]{2,3,1,0:T(8,128)}), f32[4,4,128,16]{2,3,1,0:T(8,128)S(1)}, u32[]{:S(2)}, u32[]{:S(2)}) async-start(f32[4,4,128,16]{2,3,1,0:T(8,128)} %broadcast_in_dim.11), calls=%async_computation.1 | async-start | bytes 262144 | tf_op jit(solution)/shard_map/all_to_all | solution.py:12
  148.7 5.6 %copy-start.2 = (s32[4]{0:T(128)S(1)}, s32[4]{0:T(128)}, u32[]{:S(2)}) copy-start(s32[4]{0:T(128)} %param.11) | copy-start | bytes 52
  148.7 117.6 %all-to-all-start = ((bf16[4,128,4608]{2,1,0:T(8,128)(2,1)}), bf16[4,128,4608]{2,1,0:T(8,128)(2,1)}, u32[]{:S(2)}, u32[]{:S(2)}) async-start(bf16[4,128,4608]{2,1,0:T(8,128)(2,1)} %bitcast.31), calls=%async_computation | async-start | bytes 9437184 | tf_op jit(solution)/shard_map/all_to_all | solution.py:28
Sparse Core Ops, SparseCore 0:
  9.1 127.6 all-gather.2
  138.6 109.6 all-gather.4
where the time goes:
time: 279 us; the launch traced here: 278 us
  waiting for transfers between devices  214 us (77%)
  matrix products  19.4 us (7%)
  local copies, waits for them, and re-layouts  16.5 us (6%)
  between operations  13.5 us (5%)
  starting transfers between devices  11.1 us (4%)
  other arithmetic  4.06 us (1%)
    all_gather x1, waiting for transfers between devices, body(): lax.all_gather(base_up_weight, 'gx', axis=1, tiled=True)  119 us
    all_gather x1, waiting for transfers between devices, body(): lax.all_gather(adapter_up_weight, 'gx', axis=0, tiled=True)  92.7 us
    unnamed x8, local copies, waits for them, and re-layouts  15 us
    dot_general x1, matrix products, body(): jnp.dot(tokens, lax.all_gather(base_up_weight, 'gx', axis=1, tiled=True),...  11.9 us
  transfers between devices with their start and end apart: 4, of which 2 were waited for; matrix products, arithmetic and copies ran while one was open for 13% of the time, Pallas kernels for 0%

commit v1 on v0

v1 whole, which is shorter than its diff:
```python
import functools

import jax
import jax.numpy as jnp
from jax import lax
from jax.experimental import pallas as pl
from jax.experimental.pallas import tpu as pltpu
from jax.sharding import PartitionSpec as P

BLOCK = 128
RANK = 16
CATALOG = 64
WIDTH = 1152
COLS = 288
HALF = COLS // 2
SLICE = 4 * COLS
UNITS = 16
LAG_RELAY = 2
LAG_SUM = 4
BF = jnp.bfloat16
F32 = jnp.float32
LAST = (((1,), (1,)), ((), ()))


def swap23(n):
    return n + n // 2 - 2 * (n // 3)


def unit_of(step):
    turn = (step + 3) // 4 % 4
    extra = 1 - (turn + 3) // 4
    return swap23(turn), swap23(((step + 3) % 4 + extra) % 4)


def kernel(
    idx_ref, live_ref, tok_hbm, wt_hbm, down_hbm, up_hbm, out_ref,
    toks, wts, down, up, parts, relay, arrived, sums, final,
    idx_all, idx_s, spread, picked, zpicks, chosen, upfin, shr, shr_in,
    local_sem, tok_s, tok_r, tokf_s, tokp_s, tokp_r, w_s, w_r, wf_s,
    r1_s, r1_r, r2_s, r2_r, fin_s, fin_r,
    ixa_s, ixa_r, ixb_s, ixb_r, u1_s, u1_r, u2_s, u2_r, u3_s, u3_r, sh_s, sh_r,
):
    gx = lax.axis_index("gx")
    y = lax.axis_index("gy")
    gz = lax.axis_index("gz")
    z, x = gx // 4, gx % 4
    zh, core = gz // 2, gz % 2
    ring = zh * 4 + z

    def along_x(step):
        return (z * 4 + (x + step) % 4, y, gz)

    def along_y(step):
        return (gx, (y + step) % 4, gz)

    def along_z(step):
        return (((z + step) % 4) * 4 + x, y, gz)

    def on_ring(step):
        place = (ring + step) % 8
        return ((place % 4) * 4 + x, y, (place // 4) * 2 + core)

    partner = (gx, y, zh * 2 + 1 - core)

    def remote(src, dst, send, recv, to):
        return pltpu.make_async_remote_copy(
            src_ref=src, dst_ref=dst, send_sem=send, recv_sem=recv,
            device_id=to, device_id_type=pl.DeviceIdType.MESH,
        )

    first, second = 2 * core, 2 * core + 1

    def tok_own(way, part):
        block = first if part == 0 else second
        return remote(
            tok_hbm.at[block], toks.at[3 if way > 0 else 1, block],
            tok_s.at[0 if way > 0 else 1, part], tok_r.at[2 if way > 0 else 0, part], on_ring(way),
        )

    def tok_forward(way):
        block = first if way > 0 else second
        part = 0 if way > 0 else 1
        return remote(
            toks.at[3 if way > 0 else 1, block], toks.at[2, block],
            tokf_s.at[part], tok_r.at[1, part], on_ring(way),
        )

    def tok_partner(slot, part):
        block = first if part == 0 else second
        return remote(
            toks.at[slot, block], toks.at[slot, block],
            tokp_s.at[slot - 1, part], tokp_r.at[slot - 1, part], partner,
        )

    def tok_arrival(slot, part):
        block = first if part == 0 else second
        return remote(
            toks.at[slot, block], toks.at[slot, block],
            tokp_s.at[slot - 1, part], tok_r.at[slot - 1, part], partner,
        )

    def tok_partner_arrival(slot, part):
        block = 2 * (1 - core) + part
        return remote(
            toks.at[slot, block], toks.at[slot, block],
            tokp_s.at[slot - 1, part], tokp_r.at[slot - 1, part], partner,
        )

    def w_own(way, part):
        return remote(
            wt_hbm.at[part], wts.at[3 if way > 0 else 1, part],
            w_s.at[0 if way > 0 else 1, part], w_r.at[2 if way > 0 else 0, part], along_x(way % 4),
        )

    def w_forward(way):
        part = 0 if way > 0 else 1
        return remote(
            wts.at[3 if way > 0 else 1, part], wts.at[2, part],
            wf_s.at[part], w_r.at[1, part], along_x(way % 4),
        )

    def w_arrival(slot, part):
        return remote(
            wts.at[slot, part], wts.at[slot, part],
            wf_s.at[part], w_r.at[slot - 1, part], along_x(1),
        )

    def relay_copy(step, part):
        return remote(
            parts.at[step, (y + 2) % 4, part], relay.at[step, part],
            r1_s.at[step, part], r1_r.at[step, part], along_y(1 if part == 0 else 3),
        )

    def sum_copy(step, part):
        way = 1 if part == 0 else 3
        return remote(
            parts.at[step, (y + way) % 4], arrived.at[step, part],
            r2_s.at[step, part], r2_r.at[step, part], along_y(way),
        )

    def final_copy(step):
        s, t = unit_of(step)
        chunk = (x + t) % 4
        return remote(
            sums.at[step], final.at[z, chunk], fin_s.at[step], fin_r.at[z, chunk], along_z(s)
        )

    def index_x(step):
        return remote(
            idx_all.at[z, x], idx_all.at[z, x], ixa_s.at[step - 1], ixa_r.at[step - 1], along_x(step)
        )

    def index_x_arrival(step):
        place = (x + 4 - step) % 4
        return remote(
            idx_all.at[z, place], idx_all.at[z, place],
            ixa_s.at[step - 1], ixa_r.at[step - 1], along_x(step),
        )

    def index_z(step):
        return remote(
            idx_all.at[z], idx_all.at[z], ixb_s.at[step - 1], ixb_r.at[step - 1], along_z(step)
        )

    def index_z_arrival(step):
        place = (z + 4 - step) % 4
        return remote(
            idx_all.at[place], idx_all.at[place],
            ixb_s.at[step - 1], ixb_r.at[step - 1], along_z(step),
        )

    def up_spread(step):
        columns = pl.ds(pl.multiple_of((x + step) % 4 * SLICE, SLICE), SLICE)
        return remote(
            up.at[:, :, columns], spread.at[x], u1_s.at[step - 1], u1_r.at[step - 1], along_x(step)
        )

    def up_spread_arrival(step):
        place = (x + 4 - step) % 4
        return remote(
            spread.at[place], spread.at[place], u1_s.at[step - 1], u1_r.at[step - 1], along_x(step)
        )

    def up_pick(step):
        return remote(
            picked.at[(z + step) % 4], zpicks.at[step - 1],
            u2_s.at[step - 1], u2_r.at[step - 1], along_z(step),
        )

    def up_last(step):
        return remote(
            chosen.at[(x + step) % 4], upfin.at[x], u3_s.at[step - 1], u3_r.at[step - 1], along_x(step)
        )

    def up_last_arrival(step):
        place = (x + 4 - step) % 4
        return remote(
            upfin.at[place], upfin.at[place], u3_s.at[step - 1], u3_r.at[step - 1], along_x(step)
        )

    def shrink_copy(step):
        return remote(
            shr.at[(y + step) % 4], shr_in.at[step - 1],
            sh_s.at[step - 1], sh_r.at[step - 1], along_y(step),
        )

    loads = [
        pltpu.make_async_copy(tok_hbm, toks.at[0], local_sem.at[0]),
        pltpu.make_async_copy(wt_hbm, wts.at[0], local_sem.at[1]),
        pltpu.make_async_copy(down_hbm, down, local_sem.at[2]),
        pltpu.make_async_copy(up_hbm, up, local_sem.at[3]),
    ]
    for load in loads:
        load.start()

    lane = lax.broadcasted_iota(jnp.int32, (1, 128), 1)
    row = jnp.zeros((1, 128), jnp.int32)
    for block in range(4):
        row = jnp.where(lane == block, idx_ref[block], row)
    idx_all[z, x] = row

    barrier = pltpu.get_barrier_semaphore()
    peers = [along_x(n) for n in (1, 2, 3)] + [along_y(n) for n in (1, 2, 3)]
    peers += [along_z(n) for n in (1, 2, 3)] + [on_ring(1), on_ring(-1), partner]
    for peer in peers:
        pl.semaphore_signal(barrier, inc=1, device_id=peer, device_id_type=pl.DeviceIdType.MESH)
    pl.semaphore_wait(barrier, len(peers))

    for n in (1, 2, 3):
        index_x(n).start()
    for way, order in ((1, (0, 1)), (-1, (1, 0))):
        for part in order:
            w_own(way, part).start()
            tok_own(way, part).start()

    for load in loads:
        load.wait()
    for block in range(4):
        chosen_down = down[idx_ref[block]]
        shr[block] = lax.dot_general(chosen_down, toks[0, block], LAST, preferred_element_type=F32)
    for n in (1, 2, 3):
        index_x_arrival(n).wait_recv()
    for n in (1, 2, 3):
        index_z(n).start()
        shrink_copy(n).start()

    def step_body(step, carry):
        @pl.when(step == 1)
        def _():
            tok_arrival(1, 1).wait_recv()
            tok_forward(-1).start()
            tok_partner(1, 1).start()
            tok_arrival(3, 0).wait_recv()
            tok_forward(1).start()
            tok_partner(3, 0).start()
            w_arrival(3, 0).wait_recv()
            w_forward(1).start()
            w_arrival(1, 1).wait_recv()
            w_forward(-1).start()
            for n in (1, 3, 2):
                up_spread(n).start()
            tok_arrival(1, 0).wait_recv()
            tok_partner(1, 0).start()
            tok_partner_arrival(1, 1).wait_recv()
            tok_partner_arrival(1, 0).wait_recv()

        @pl.when(step == 2)
        def _():
            tok_arrival(3, 1).wait_recv()
            tok_partner(3, 1).start()
            w_arrival(1, 0).wait_recv()

        @pl.when(step == 3)
        def _():
            w_arrival(3, 1).wait_recv()

        @pl.when(step == 4)
        def _():
            w_arrival(2, 0).wait_recv()
            w_arrival(2, 1).wait_recv()

        @pl.when(step == 5)
        def _():
            tok_partner_arrival(3, 0).wait_recv()
            tok_partner_arrival(3, 1).wait_recv()

        @pl.when(step == 6)
        def _():
            for part in (0, 1):
                tok_arrival(2, part).wait_recv()
                tok_partner(2, part).start()

        @pl.when(step == 9)
        def _():
            for part in (0, 1):
                tok_partner_arrival(2, part).wait_recv()

        @pl.when(step < UNITS)
        def _():
            s, t = unit_of(step)
            result = lax.dot_general(
                wts[t].reshape(COLS, WIDTH), toks[s].reshape(4 * BLOCK, WIDTH), LAST,
                preferred_element_type=F32,
            ).astype(BF)
            for block in range(4):
                tile = result[:, block * BLOCK : (block + 1) * BLOCK]
                parts[step, block] = tile.reshape(2, HALF, BLOCK)

        @pl.when((step >= LAG_RELAY) & (step < UNITS + LAG_RELAY))
        def _():
            done = step - LAG_RELAY
            for part in (0, 1):
                to = (y + (1 if part == 0 else 3)) % 4
                relay_copy(done, part).wait_recv()
                added = parts[done, to, part].astype(F32) + relay[done, part].astype(F32)
                parts[done, to, part] = added.astype(BF)

        @pl.when(step < UNITS)
        def _():
            for part in (0, 1):
                relay_copy(step, part).start()

        @pl.when((step >= LAG_RELAY) & (step < UNITS + LAG_RELAY))
        def _():
            for part in (0, 1):
                sum_copy(step - LAG_RELAY, part).start()

        @pl.when(step >= LAG_SUM)
        def _():
            done = step - LAG_SUM
            s, t = unit_of(done)
            for part in (0, 1):
                sum_copy(done, part).wait_recv()
            total = parts[done, y].astype(F32) + arrived[done, 0].astype(F32)
            total = (total + arrived[done, 1].astype(F32)).astype(BF)

            @pl.when(s == 0)
            def _():
                final[z, (x + t) % 4] = total

            @pl.when(s > 0)
            def _():
                sums[done] = total
                final_copy(done).start()

        @pl.when(step == 7)
        def _():
            for n in (1, 2, 3):
                index_z_arrival(n).wait_recv()
            to_scalars = pltpu.make_async_copy(idx_all, idx_s, local_sem.at[0])
            to_scalars.start()
            own = pltpu.make_async_copy(
                up.at[:, :, pl.ds(pl.multiple_of(x * SLICE, SLICE), SLICE)], spread.at[x], local_sem.at[1]
            )
            own.start()
            for n in (1, 2, 3):
                up_spread_arrival(n).wait_recv()
            to_scalars.wait()
            own.wait()
            for to_z in range(4):
                for to_x in range(4):
                    local = idx_s[to_z, to_x, 0, y] - 16 * z
                    owned = jnp.where((local >= 0) & (local < 16), 1.0, 0.0).astype(F32)
                    kept = jnp.clip(local, 0, 15)
                    factor = spread[kept // 4, kept % 4].astype(F32) * owned
                    picked[to_z, to_x] = factor.astype(BF)
            for n in (1, 2, 3):
                up_pick(n).start()

        @pl.when(step == 12)
        def _():
            for n in (1, 2, 3):
                up_pick(n).wait_recv()
            for to_x in range(4):
                chosen[to_x] = (picked[z, to_x] + zpicks[0, to_x]) + (zpicks[1, to_x] + zpicks[2, to_x])
            for n in (1, 2, 3):
                up_last(n).start()
            upfin[x] = chosen[x]

        return carry

    lax.fori_loop(0, UNITS + LAG_SUM, step_body, 0)

    for n in (1, 2, 3):
        shrink_copy(n).wait_recv()
    low = (shr[y] + shr_in[0] + (shr_in[1] + shr_in[2])).astype(BF)
    same = lax.broadcasted_iota(jnp.int32, (BLOCK, BLOCK), 0) == lax.broadcasted_iota(
        jnp.int32, (BLOCK, BLOCK), 1
    )
    eye = jnp.where(same, 1.0, 0.0).astype(BF)
    turned = lax.dot_general(eye, low, LAST, preferred_element_type=F32)
    doubled = (2.0 * turned).astype(BF)
    rows = lax.broadcasted_iota(jnp.int32, (BLOCK, 1), 0)
    live = rows < live_ref[y]

    for n in (1, 2, 3):
        up_last_arrival(n).wait_recv()
        for t in range(4):
            place = (z + n) % 4
            remote(
                sums.at[0], final.at[place, t], fin_s.at[0], fin_r.at[place, t], along_z(n)
            ).wait_recv()
    for part in range(4):
        base = lax.dot_general(
            eye, final[part].reshape(SLICE, BLOCK), LAST, preferred_element_type=F32
        )
        extra = jnp.dot(doubled, upfin[part], preferred_element_type=F32)
        out_ref[:, part * SLICE : (part + 1) * SLICE] = jnp.where(live, base + extra, 0.0).astype(BF)

    for n in (1, 2, 3):
        index_x(n).wait_send()
        index_z(n).wait_send()
        up_spread(n).wait_send()
        up_pick(n).wait_send()
        up_last(n).wait_send()
        shrink_copy(n).wait_send()
    for way in (1, -1):
        for part in (0, 1):
            w_own(way, part).wait_send()
            tok_own(way, part).wait_send()
        w_forward(way).wait_send()
        tok_forward(way).wait_send()
    for slot in (1, 2, 3):
        for part in (0, 1):
            tok_partner(slot, part).wait_send()

    def drain(step, carry):
        for part in (0, 1):
            relay_copy(step, part).wait_send()
            sum_copy(step, part).wait_send()

        @pl.when(unit_of(step)[0] > 0)
        def _():
            final_copy(step).wait_send()

        return carry

    lax.fori_loop(0, UNITS, drain, 0)


def body(tokens, base_up_weight, adapter_down_weight, adapter_up_weight, block_adapter_index, request_rows):
    dma = pltpu.SemaphoreType.DMA
    half_tile = (2, HALF, BLOCK)
    any_space = pl.BlockSpec(memory_space=pl.ANY)
    scalars = pl.BlockSpec(memory_space=pltpu.SMEM)
    return pl.pallas_call(
        kernel,
        out_shape=jax.ShapeDtypeStruct((BLOCK, 4 * SLICE), BF),
        in_specs=[scalars, scalars, any_space, any_space, any_space, any_space],
        out_specs=pl.BlockSpec(memory_space=pltpu.VMEM),
        scratch_shapes=[
            pltpu.VMEM((4, 4, BLOCK, WIDTH), BF),
            pltpu.VMEM((4, 2, HALF, WIDTH), BF),
            pltpu.VMEM((CATALOG, RANK, WIDTH), BF),
            pltpu.VMEM((4, RANK, 4 * SLICE), BF),
            pltpu.VMEM((UNITS, 4, *half_tile), BF),
            pltpu.VMEM((UNITS, *half_tile), BF),
            pltpu.VMEM((UNITS, 2, *half_tile), BF),
            pltpu.VMEM((UNITS, *half_tile), BF),
            pltpu.VMEM((4, 4, *half_tile), BF),
            pltpu.VMEM((4, 4, 1, 128), jnp.int32),
            pltpu.SMEM((4, 4, 1, 128), jnp.int32),
            pltpu.VMEM((4, 4, RANK, SLICE), BF),
            pltpu.VMEM((4, 4, RANK, SLICE), BF),
            pltpu.VMEM((3, 4, RANK, SLICE), BF),
            pltpu.VMEM((4, RANK, SLICE), BF),
            pltpu.VMEM((4, RANK, SLICE), BF),
            pltpu.VMEM((4, RANK, BLOCK), F32),
            pltpu.VMEM((3, RANK, BLOCK), F32),
            dma((4,)),
            dma((2, 2)), dma((3, 2)), dma((2,)), dma((3, 2)), dma((3, 2)),
            dma((2, 2)), dma((3, 2)), dma((2,)),
            dma((UNITS, 2)), dma((UNITS, 2)), dma((UNITS, 2)), dma((UNITS, 2)),
            dma((UNITS,)), dma((4, 4)),
            dma((3,)), dma((3,)), dma((3,)), dma((3,)),
            dma((3,)), dma((3,)), dma((3,)), dma((3,)), dma((3,)), dma((3,)),
            dma((3,)), dma((3,)),
        ],
        compiler_params=pltpu.CompilerParams(
            collective_id=0, has_side_effects=True, vmem_limit_bytes=50 * 1024 * 1024
        ),
    )(
        block_adapter_index,
        request_rows,
        tokens.reshape(4, BLOCK, WIDTH),
        base_up_weight.T.reshape(2, HALF, WIDTH),
        adapter_down_weight,
        adapter_up_weight,
    )


def solution(mesh):
    in_specs = (
        P("gx", "gy"),
        P("gy", ("gz", "gx")),
        P(None, None, "gy"),
        P("gx", None, "gz"),
        P("gx"),
        P("gx"),
    )
    out_specs = P(("gx", "gy"), "gz")
    return jax.shard_map(body, mesh=mesh, in_specs=in_specs, out_specs=out_specs, check_vma=False)
```

time: 279 us -> 87.3 us (0.31)
  the two profiles are of different devices: /device:TPU:8 before, /device:TPU:224 now
where the time goes in v1:
time: 87.3 us; the launch traced here: 87.1 us
  Pallas kernels  81.3 us (93%)
  local copies, waits for them, and re-layouts  5.75 us (7%)
    pallas_call x1, Pallas kernels, body(): pl.pallas_call(kernel, out_shape=jax.ShapeDtypeStruct((BLOCK, 4 * SLICE),...  81.3 us
    unnamed x11, local copies, waits for them, and re-layouts  5.75 us

profile of v1, /device:TPU:224, one launch (start us, length us, event | category | flops | bytes accessed | tf_op | source)
XLA Modules:
  0.0 87.1 jit_solution(2427207273161929918)
XLA Ops:
  0.0 0.0 copy-start
  0.0 1.3 %copy-done = bf16[512,1152]{1,0:T(8,128)(2,1)S(1)} copy-done((bf16[512,1152]{1,0:T(8,128)(2,1)S(1)}, bf16[512,1152]{1,0:T(8,128)(2,1)}, u32[]{:S(2)}) %copy-start) | copy-done | bytes 1179672
  1.3 0.0 copy-start.1
  1.3 1.1 %copy-done.1 = bf16[1152,288]{0,1:T(8,128)(2,1)S(1)} copy-done((bf16[1152,288]{0,1:T(8,128)(2,1)S(1)}, bf16[1152,288]{0,1:T(8,128)(2,1)}, u32[]{:S(2)}) %copy-start.1) | copy-done | bytes 663576
  2.4 0.0 copy-start.2
  2.4 1.1 %copy-done.2 = bf16[4,16,4608]{2,1,0:T(8,128)(2,1)S(1)} copy-done((bf16[4,16,4608]{2,1,0:T(8,128)(2,1)S(1)}, bf16[4,16,4608]{2,1,0:T(8,128)(2,1)}, u32[]{:S(2)}) %copy-start.2) | copy-done | bytes 589848
  3.4 0.0 copy-start.3
  3.4 0.7 copy-done.3
  4.1 0.0 copy-start.4
  4.1 0.7 copy-done.4
  4.7 81.3 %shard_map.64 = bf16[128,4608]{1,0:T(8,128)(2,1)S(1)} custom-call(s32[4]{0:T(128)S(1)} %copy-done.3, s32[4]{0:T(128)S(1)} %copy-done.4, bf16[4,128,1152]{2,1,0:T(8,128)(2,1)S(1)} %bitcast.4, bf16[2,144,1152]{2,1,0:T(8,128)(2,1)S(1)} %bitcast.5, bf16[64,16,1152]{2,1,0:T(8,128)(2,1)} %down_hbm.1, bf16[4,16,4608]{2,1,0:T(8,128)(2,1)S(1)} %copy-done.2), custom_call_target="tpu_custom_call" | custom-call | tf_op jit(solution)/shard_map/pallas_call | solution.py:446
  86.1 1.0 %copy.8 = bf16[128,4608]{1,0:T(8,128)(2,1)} copy(bf16[128,4608]{1,0:T(8,128)(2,1)S(1)} %shard_map.64) | data formatting | bytes 2359296
Async XLA Ops:
  0.0 1.3 %copy-start = (bf16[512,1152]{1,0:T(8,128)(2,1)S(1)}, bf16[512,1152]{1,0:T(8,128)(2,1)}, u32[]{:S(2)}) copy-start(bf16[512,1152]{1,0:T(8,128)(2,1)} %param.6) | copy-start | bytes 3538948
  1.3 1.1 %copy-start.1 = (bf16[1152,288]{0,1:T(8,128)(2,1)S(1)}, bf16[1152,288]{0,1:T(8,128)(2,1)}, u32[]{:S(2)}) copy-start(bf16[1152,288]{0,1:T(8,128)(2,1)} %param.7) | copy-start | bytes 1990660
  2.4 1.1 %copy-start.2 = (bf16[4,16,4608]{2,1,0:T(8,128)(2,1)S(1)}, bf16[4,16,4608]{2,1,0:T(8,128)(2,1)}, u32[]{:S(2)}) copy-start(bf16[4,16,4608]{2,1,0:T(8,128)(2,1)} %up_hbm.1) | copy-start | bytes 1769476
  3.4 0.7 copy-start.3
  4.1 0.7 copy-start.4

commit v2 on v1

v2 whole, which is shorter than its diff:
```python
import functools

import jax
import jax.numpy as jnp
from jax import lax
from jax.experimental import pallas as pl
from jax.experimental.pallas import tpu as pltpu
from jax.sharding import PartitionSpec as P

BLOCK = 128
RANK = 16
CATALOG = 64
WIDTH = 1152
COLS = 288
HALF = COLS // 2
SLICE = 4 * COLS
UNITS = 16
LAG_RELAY = 2
LAG_SUM = 4
PICK_STEP = 8
PAIR_STEP = 11
FAR_STEP = 16
BF = jnp.bfloat16
F32 = jnp.float32
LAST = (((1,), (1,)), ((), ()))


ORDER = (
    (0, 0), (1, 0), (1, 1), (0, 1), (1, 2), (2, 0), (2, 1), (2, 2),
    (3, 0), (3, 1), (3, 2), (1, 3), (2, 3), (3, 3), (0, 2), (0, 3),
)


def staircase(step, column):
    rises = [(at, ORDER[at][column] - ORDER[at - 1][column]) for at in range(1, UNITS)]
    return sum(rise * ((step + 16 - at) // 16) for at, rise in rises if rise)


def unit_of(step):
    return staircase(step, 0), staircase(step, 1)


def places_on(kind, part):
    three = kind // 3
    two = kind // 2 - three
    one = kind - 2 * (kind // 2) - three
    return one * (3 - 2 * part) + two * (1 + 2 * part) + 2 * three


def kernel(
    idx_hbm, live_hbm, tok_hbm, wt_hbm, down_hbm, up_hbm, out_hbm,
    toks, wts, down, up, parts, relay, arrived, sums, final, upfin, out,
    idx_ref, live_ref, idx_all, idx_s, spread, transit, picked, zpicks, chosen, shr, shr_in,
    local_sem, out_sem, tok_s, tok_r, tokp_s, tokp_r, w_s, w_r,
    r1_s, r1_r, r2_s, r2_r, fin_s, fin_r,
    ixa_s, ixa_r, ixb_s, ixb_r, u1_s, u1_r, u2_s, u2_r, u3_s, u3_r, sh_s, sh_r,
):
    gx = lax.axis_index("gx")
    y = lax.axis_index("gy")
    gz = lax.axis_index("gz")
    z, x = gx // 4, gx % 4
    zh, core = gz // 2, gz % 2
    ring = zh * 4 + z

    def along_x(step):
        return (z * 4 + (x + step) % 4, y, gz)

    def along_y(step):
        return (gx, (y + step) % 4, gz)

    def along_z(step):
        return (((z + step) % 4) * 4 + x, y, gz)

    def on_ring(step):
        place = (ring + step) % 8
        return ((place % 4) * 4 + x, y, (place // 4) * 2 + core)

    partner = (gx, y, zh * 2 + 1 - core)

    def remote(src, dst, send, recv, to):
        return pltpu.make_async_remote_copy(
            src_ref=src, dst_ref=dst, send_sem=send, recv_sem=recv,
            device_id=to, device_id_type=pl.DeviceIdType.MESH,
        )

    def kind_of(way, part):
        return 1 if (way > 0) == (part == 0) else 2

    def tok_own(way, part):
        kind, block = kind_of(way, part), 2 * core + part
        return remote(
            toks.at[0, block], toks.at[kind, block],
            tok_s.at[kind - 1, part], tok_r.at[kind - 1, part], on_ring(way),
        )

    def tok_forward(part):
        block = 2 * core + part
        return remote(
            toks.at[1, block], toks.at[3, block],
            tok_s.at[2, part], tok_r.at[2, part], on_ring(1 if part == 0 else -1),
        )

    def tok_partner(kind, part, sent=True):
        block = 2 * (core if sent else 1 - core) + part
        return remote(
            toks.at[kind, block], toks.at[kind, block],
            tokp_s.at[kind - 1, part], tokp_r.at[kind - 1, part], partner,
        )

    def tok_arrival(kind, part):
        block = 2 * core + part
        return remote(
            toks.at[kind, block], toks.at[kind, block],
            tok_s.at[kind - 1, part], tok_r.at[kind - 1, part], partner,
        )

    def tok_partner_arrival(kind, part):
        return tok_partner(kind, part, False)

    def w_own(way, part):
        kind = kind_of(way, part)
        return remote(
            wts.at[0, part], wts.at[kind, part],
            w_s.at[kind - 1, part], w_r.at[kind - 1, part], along_x(way % 4),
        )

    def w_forward(part):
        return remote(
            wts.at[1, part], wts.at[3, part],
            w_s.at[2, part], w_r.at[2, part], along_x(1 if part == 0 else 3),
        )

    def w_arrival(kind, part):
        return remote(
            wts.at[kind, part], wts.at[kind, part],
            w_s.at[kind - 1, part], w_r.at[kind - 1, part], along_x(1),
        )

    def relay_copy(step, part):
        return remote(
            parts.at[step, (y + 2) % 4, part], relay.at[step, part],
            r1_s.at[step, part], r1_r.at[step, part], along_y(1 if part == 0 else 3),
        )

    def sum_copy(step, part):
        way = 1 if part == 0 else 3
        return remote(
            parts.at[step, (y + way) % 4], arrived.at[step, part],
            r2_s.at[step, part], r2_r.at[step, part], along_y(way),
        )

    def final_copy(step, part):
        rows, columns = unit_of(step)
        chunk = (x + places_on(columns, part)) % 4
        return remote(
            sums.at[step, part], final.at[z, chunk, part],
            fin_s.at[step, part], fin_r.at[z, chunk, part], along_z(places_on(rows, y % 2)),
        )

    def final_arrival(place, chunk, part):
        return remote(
            final.at[place, chunk, part], final.at[place, chunk, part],
            fin_s.at[0, part], fin_r.at[place, chunk, part], along_z(1),
        )

    def index_x(step):
        return remote(
            idx_all.at[z, x], idx_all.at[z, x], ixa_s.at[step - 1], ixa_r.at[step - 1], along_x(step)
        )

    def index_x_arrival(step):
        place = (x + 4 - step) % 4
        return remote(
            idx_all.at[z, place], idx_all.at[z, place],
            ixa_s.at[step - 1], ixa_r.at[step - 1], along_x(step),
        )

    def index_z(step):
        return remote(
            idx_all.at[z], idx_all.at[z], ixb_s.at[step - 1], ixb_r.at[step - 1], along_z(step)
        )

    def index_z_arrival(step):
        place = (z + 4 - step) % 4
        return remote(
            idx_all.at[place], idx_all.at[place],
            ixb_s.at[step - 1], ixb_r.at[step - 1], along_z(step),
        )

    def up_columns(step):
        return pl.ds(pl.multiple_of((x + step) % 4 * SLICE, SLICE), SLICE)

    def up_near(step):
        which = step // 2
        return remote(
            up.at[:, :, up_columns(step)], spread.at[x], u1_s.at[which], u1_r.at[which], along_x(step)
        )

    def up_near_arrival(step):
        which, place = step // 2, (x + 4 - step) % 4
        return remote(
            spread.at[place], spread.at[place], u1_s.at[which], u1_r.at[which], along_x(step)
        )

    def up_cross(part):
        return remote(
            up.at[pl.ds(2 * part, 2), :, up_columns(2)], transit.at[part],
            u1_s.at[2 + part], u1_r.at[2 + part], along_x(1 if part == 0 else 3),
        )

    def up_relay(part):
        step = 1 if part == 0 else 3
        place = (x + 4 - step) % 4
        return remote(
            transit.at[part], spread.at[place, pl.ds(2 * part, 2)],
            u1_s.at[4 + part], u1_r.at[4 + part], along_x(step),
        )

    mate = 1 - 2 * (z % 2)
    far = 3 - 2 * z

    def up_pair(part):
        chunk = z + mate if part == 0 else 3 - (z + mate)
        return remote(
            picked.at[chunk], zpicks.at[part], u2_s.at[part], u2_r.at[part], along_z(mate + 4)
        )

    def up_far():
        return remote(picked.at[3 - z], zpicks.at[2], u2_s.at[2], u2_r.at[2], along_z(far + 4))

    def up_last(step):
        return remote(
            chosen.at[(x + step) % 4], upfin.at[x], u3_s.at[step - 1], u3_r.at[step - 1], along_x(step)
        )

    def up_last_arrival(step):
        place = (x + 4 - step) % 4
        return remote(
            upfin.at[place], upfin.at[place], u3_s.at[step - 1], u3_r.at[step - 1], along_x(step)
        )

    def shrink_copy(step):
        return remote(
            shr.at[(y + step) % 4], shr_in.at[step - 1],
            sh_s.at[step - 1], sh_r.at[step - 1], along_y(step),
        )

    loads = [
        pltpu.make_async_copy(idx_hbm, idx_ref, local_sem.at[4]),
        pltpu.make_async_copy(tok_hbm, toks.at[0], local_sem.at[0]),
        pltpu.make_async_copy(wt_hbm, wts.at[0], local_sem.at[1]),
        pltpu.make_async_copy(down_hbm, down, local_sem.at[2]),
        pltpu.make_async_copy(up_hbm, up, local_sem.at[3]),
        pltpu.make_async_copy(live_hbm, live_ref, local_sem.at[5]),
    ]
    for load in loads:
        load.start()
    barrier = pltpu.get_barrier_semaphore()
    peers = [along_x(n) for n in (1, 2, 3)] + [along_y(n) for n in (1, 2, 3)]
    peers += [along_z(n) for n in (1, 2, 3)] + [on_ring(1), on_ring(-1), partner]
    for peer in peers:
        pl.semaphore_signal(barrier, inc=1, device_id=peer, device_id_type=pl.DeviceIdType.MESH)

    loads[0].wait()
    lane = lax.broadcasted_iota(jnp.int32, (1, 128), 1)
    row = jnp.zeros((1, 128), jnp.int32)
    for block in range(4):
        row = jnp.where(lane == block, idx_ref[block], row)
    idx_all[z, x] = row
    loads[1].wait()
    loads[2].wait()
    pl.semaphore_wait(barrier, len(peers))

    for n in (1, 2, 3):
        index_x(n).start()
    for way, order in ((1, (0, 1)), (-1, (1, 0))):
        for part in order:
            w_own(way, part).start()
            tok_own(way, part).start()

    def step_body(step, carry):
        @pl.when(step == 1)
        def _():
            loads[3].wait()
            for block in range(4):
                chosen_down = down[idx_ref[block]]
                shr[block] = lax.dot_general(
                    chosen_down, toks[0, block], LAST, preferred_element_type=F32
                )
            for n in (1, 2, 3):
                index_x_arrival(n).wait_recv()
            for n in (1, 2, 3):
                index_z(n).start()
                shrink_copy(n).start()
            for part in (0, 1):
                tok_arrival(1, part).wait_recv()
                tok_partner(1, part).start()
            for part in (0, 1):
                tok_partner_arrival(1, part).wait_recv()

        @pl.when(step == 2)
        def _():
            for part in (0, 1):
                w_arrival(1, part).wait_recv()

        @pl.when(step == 4)
        def _():
            for part in (0, 1):
                tok_arrival(2, part).wait_recv()
                tok_forward(part).start()
                tok_partner(2, part).start()
            loads[4].wait()
            for part in (0, 1):
                w_arrival(2, part).wait_recv()
            for part in (0, 1):
                up_near(1 + 2 * part).start()
                up_cross(part).start()

        @pl.when(step == 5)
        def _():
            for part in (0, 1):
                tok_partner_arrival(2, part).wait_recv()

        @pl.when(step == 6)
        def _():
            for part in (0, 1):
                up_cross(part).wait_recv()
                up_relay(part).start()
            for part in (0, 1):
                w_forward(part).start()

        @pl.when(step == 7)
        def _():
            for part in (0, 1):
                tok_arrival(3, part).wait_recv()
                tok_partner(3, part).start()

        @pl.when(step == 8)
        def _():
            for part in (0, 1):
                tok_partner_arrival(3, part).wait_recv()

        @pl.when(step == 11)
        def _():
            for part in (0, 1):
                w_arrival(3, part).wait_recv()

        @pl.when(step < UNITS)
        def _():
            s, t = unit_of(step)
            result = lax.dot_general(
                wts[t].reshape(COLS, WIDTH), toks[s].reshape(4 * BLOCK, WIDTH), LAST,
                preferred_element_type=F32,
            ).astype(BF)
            for block in range(4):
                tile = result[:, block * BLOCK : (block + 1) * BLOCK]
                parts[step, block] = tile.reshape(2, HALF, BLOCK)

        @pl.when((step >= LAG_RELAY) & (step < UNITS + LAG_RELAY))
        def _():
            done = step - LAG_RELAY
            for part in (0, 1):
                to = (y + (1 if part == 0 else 3)) % 4
                relay_copy(done, part).wait_recv()
                added = parts[done, to, part].astype(F32) + relay[done, part].astype(F32)
                parts[done, to, part] = added.astype(BF)

        @pl.when(step < UNITS)
        def _():
            for part in (0, 1):
                relay_copy(step, part).start()

        @pl.when((step >= LAG_RELAY) & (step < UNITS + LAG_RELAY))
        def _():
            for part in (0, 1):
                sum_copy(step - LAG_RELAY, part).start()

        @pl.when(step >= LAG_SUM)
        def _():
            done = step - LAG_SUM
            rows, columns = unit_of(done)
            for part in (0, 1):
                sum_copy(done, part).wait_recv()
            total = parts[done, y].astype(F32) + arrived[done, 0].astype(F32)
            total = (total + arrived[done, 1].astype(F32)).astype(BF)

            @pl.when(rows == 0)
            def _():
                for part in (0, 1):
                    final[z, (x + places_on(columns, part)) % 4, part] = total[part]

            @pl.when(rows > 0)
            def _():
                sums[done] = total
                for part in (0, 1):
                    final_copy(done, part).start()

        @pl.when(step == PICK_STEP)
        def _():
            for n in (1, 2, 3):
                index_z_arrival(n).wait_recv()
            to_scalars = pltpu.make_async_copy(idx_all, idx_s, local_sem.at[0])
            to_scalars.start()
            own = pltpu.make_async_copy(
                up.at[:, :, pl.ds(pl.multiple_of(x * SLICE, SLICE), SLICE)], spread.at[x], local_sem.at[1]
            )
            own.start()
            for part in (0, 1):
                up_near_arrival(1 + 2 * part).wait_recv()
                up_relay(part).wait_recv()
            to_scalars.wait()
            own.wait()
            for to_z in range(4):
                for to_x in range(4):
                    local = idx_s[to_z, to_x, 0, y] - 16 * z
                    owned = jnp.where((local >= 0) & (local < 16), 1.0, 0.0).astype(F32)
                    kept = jnp.clip(local, 0, 15)
                    factor = spread[kept // 4, kept % 4].astype(F32) * owned
                    picked[to_z, to_x] = factor.astype(BF)
            for part in (1, 0):
                up_pair(part).start()

        @pl.when(step == PAIR_STEP)
        def _():
            up_pair(1).wait_recv()
            for to_x in range(4):
                picked[3 - z, to_x] = picked[3 - z, to_x] + zpicks[1, to_x]
            up_far().start()

        @pl.when(step == FAR_STEP)
        def _():
            up_pair(0).wait_recv()
            up_far().wait_recv()
            for to_x in range(4):
                chosen[to_x] = (picked[z, to_x] + zpicks[0, to_x]) + zpicks[2, to_x]
            for n in (1, 2, 3):
                up_last(n).start()
            upfin[x] = chosen[x]

        return carry

    lax.fori_loop(0, UNITS + LAG_SUM, step_body, 0)

    def finish_sends():
        for n in (1, 2, 3):
            index_x(n).wait_send()
            index_z(n).wait_send()
            up_last(n).wait_send()
            shrink_copy(n).wait_send()
        up_pair(0).wait_send()
        up_pair(1).wait_send()
        up_far().wait_send()
        for part in (0, 1):
            for way in (1, -1):
                w_own(way, part).wait_send()
                tok_own(way, part).wait_send()
            w_forward(part).wait_send()
            tok_forward(part).wait_send()
            up_near(1 + 2 * part).wait_send()
            up_cross(part).wait_send()
            up_relay(part).wait_send()
            for kind in (1, 2, 3):
                tok_partner(kind, part).wait_send()

        def drain(step, carry):
            for part in (0, 1):
                relay_copy(step, part).wait_send()
                sum_copy(step, part).wait_send()

                @pl.when(unit_of(step)[0] > 0)
                def _():
                    final_copy(step, part).wait_send()

            return carry

        lax.fori_loop(0, UNITS, drain, 0)

    for n in (1, 2, 3):
        shrink_copy(n).wait_recv()
    low = (shr[y] + shr_in[0] + (shr_in[1] + shr_in[2])).astype(BF)
    same = lax.broadcasted_iota(jnp.int32, (BLOCK, BLOCK), 0) == lax.broadcasted_iota(
        jnp.int32, (BLOCK, BLOCK), 1
    )
    eye = jnp.where(same, 1.0, 0.0).astype(BF)
    turned = lax.dot_general(eye, low, LAST, preferred_element_type=F32)
    doubled = (2.0 * turned).astype(BF)
    loads[5].wait()
    live = lax.broadcasted_iota(jnp.int32, (BLOCK, 1), 0) < live_ref[y]
    for n in (1, 2, 3):
        up_last_arrival(n).wait_recv()

    def write_out(n):
        place = (z + n) % 4
        columns = pl.ds(pl.multiple_of(place * SLICE, SLICE), SLICE)
        return pltpu.make_async_copy(out.at[n], out_hbm.at[:, columns], out_sem.at[n])

    for n in (0, 1, 3, 2):
        place = (z + n) % 4
        if n:
            for chunk in range(4):
                for part in (0, 1):
                    final_arrival(place, chunk, part).wait_recv()
        base = lax.dot_general(
            eye, final[place].reshape(SLICE, BLOCK), LAST, preferred_element_type=F32
        )
        extra = jnp.dot(doubled, upfin[place], preferred_element_type=F32)
        out[n] = jnp.where(live, base + extra, 0.0).astype(BF)
        write_out(n).start()
        if n == 0:
            finish_sends()
    for n in range(4):
        write_out(n).wait()


def body(tokens, base_up_weight, adapter_down_weight, adapter_up_weight, block_adapter_index, request_rows):
    dma = pltpu.SemaphoreType.DMA
    half_tile = (2, HALF, BLOCK)
    any_space = pl.BlockSpec(memory_space=pl.ANY)
    return pl.pallas_call(
        kernel,
        out_shape=jax.ShapeDtypeStruct((BLOCK, 4 * SLICE), BF),
        in_specs=[any_space] * 6,
        out_specs=any_space,
        scratch_shapes=[
            pltpu.VMEM((4, 4, BLOCK, WIDTH), BF),
            pltpu.VMEM((4, 2, HALF, WIDTH), BF),
            pltpu.VMEM((CATALOG, RANK, WIDTH), BF),
            pltpu.VMEM((4, RANK, 4 * SLICE), BF),
            pltpu.VMEM((UNITS, 4, *half_tile), BF),
            pltpu.VMEM((UNITS, *half_tile), BF),
            pltpu.VMEM((UNITS, 2, *half_tile), BF),
            pltpu.VMEM((UNITS, *half_tile), BF),
            pltpu.VMEM((4, 4, *half_tile), BF),
            pltpu.VMEM((4, RANK, SLICE), BF),
            pltpu.VMEM((4, BLOCK, SLICE), BF),
            pltpu.SMEM((4,), jnp.int32),
            pltpu.SMEM((4,), jnp.int32),
            pltpu.VMEM((4, 4, 1, 128), jnp.int32),
            pltpu.SMEM((4, 4, 1, 128), jnp.int32),
            pltpu.VMEM((4, 4, RANK, SLICE), BF),
            pltpu.VMEM((2, 2, RANK, SLICE), BF),
            pltpu.VMEM((4, 4, RANK, SLICE), BF),
            pltpu.VMEM((3, 4, RANK, SLICE), BF),
            pltpu.VMEM((4, RANK, SLICE), BF),
            pltpu.VMEM((4, RANK, BLOCK), F32),
            pltpu.VMEM((3, RANK, BLOCK), F32),
            dma((6,)), dma((4,)),
            dma((3, 2)), dma((3, 2)), dma((3, 2)), dma((3, 2)), dma((3, 2)), dma((3, 2)),
            dma((UNITS, 2)), dma((UNITS, 2)), dma((UNITS, 2)), dma((UNITS, 2)),
            dma((UNITS, 2)), dma((4, 4, 2)),
            dma((3,)), dma((3,)), dma((3,)), dma((3,)),
            dma((6,)), dma((6,)), dma((3,)), dma((3,)), dma((3,)), dma((3,)),
            dma((3,)), dma((3,)),
        ],
        compiler_params=pltpu.CompilerParams(
            collective_id=0, has_side_effects=True, vmem_limit_bytes=67043328
        ),
    )(
        block_adapter_index,
        request_rows,
        tokens.reshape(4, BLOCK, WIDTH),
        base_up_weight.T.reshape(2, HALF, WIDTH),
        adapter_down_weight,
        adapter_up_weight,
    )


def solution(mesh):
    in_specs = (
        P("gx", "gy"),
        P("gy", ("gz", "gx")),
        P(None, None, "gy"),
        P("gx", None, "gz"),
        P("gx"),
        P("gx"),
    )
    out_specs = P(("gx", "gy"), "gz")
    return jax.shard_map(body, mesh=mesh, in_specs=in_specs, out_specs=out_specs, check_vma=False)
```

time: 87.3 us -> 76 us (0.87)
  the two profiles are of different devices: /device:TPU:224 before, /device:TPU:64 now
where the time goes in v2:
time: 76 us; the launch traced here: 75.8 us
  Pallas kernels  73.5 us (97%)
  local copies, waits for them, and re-layouts  2.36 us (3%)
    pallas_call x1, Pallas kernels, body(): pl.pallas_call(kernel, out_shape=jax.ShapeDtypeStruct((BLOCK, 4 * SLICE),...  73.5 us
    unnamed x1, local copies, waits for them, and re-layouts  2.36 us

profile of v2, /device:TPU:64, one launch (start us, length us, event | category | flops | bytes accessed | tf_op | source)
XLA Modules:
  0.0 75.8 jit_solution(11248862980701128547)
XLA Ops:
  0.0 73.5 %shard_map.64 = bf16[128,4608]{1,0:T(8,128)(2,1)} custom-call(s32[4]{0:T(128)} %idx_hbm.1, s32[4]{0:T(128)} %live_hbm.1, bf16[4,128,1152]{2,1,0:T(8,128)(2,1)} %bitcast.4, bf16[2,144,1152]{2,1,0:T(8,128)(2,1)} %bitcast.5, bf16[64,16,1152]{2,1,0:T(8,128)(2,1)} %down_hbm.1, bf16[4,16,4608]{2,1,0:T(8,128)(2,1)} %up_hbm.1), custom_call_target="tpu_custom_call" | custom-call | tf_op jit(solution)/shard_map/pallas_call | solution.py:519
  73.5 2.4 %copy.8 = bf16[128,4608]{1,0:T(8,128)(2,1)} copy(bf16[128,4608]{1,0:T(8,128)(2,1)} %shard_map.64) | data formatting | bytes 2359296

commit v3 on v2

--- a/solution.py
+++ b/solution.py
@@ -17,17 +17,17 @@
 UNITS = 16
 LAG_RELAY = 2
 LAG_SUM = 4
-PICK_STEP = 8
-PAIR_STEP = 11
-FAR_STEP = 16
+PICK_STEP = 6
+PAIR_STEP = 8
+FAR_STEP = 12
 BF = jnp.bfloat16
 F32 = jnp.float32
 LAST = (((1,), (1,)), ((), ()))
 
 
 ORDER = (
-    (0, 0), (1, 0), (1, 1), (0, 1), (1, 2), (2, 0), (2, 1), (2, 2),
-    (3, 0), (3, 1), (3, 2), (1, 3), (2, 3), (3, 3), (0, 2), (0, 3),
+    (0, 0), (0, 1), (1, 0), (1, 1), (2, 0), (2, 1), (1, 2), (3, 0),
+    (2, 2), (3, 1), (1, 3), (3, 2), (2, 3), (3, 3), (0, 2), (0, 3),
 )
 
 
@@ -273,12 +273,47 @@
 
     for n in (1, 2, 3):
         index_x(n).start()
-    for way, order in ((1, (0, 1)), (-1, (1, 0))):
-        for part in order:
-            w_own(way, part).start()
-            tok_own(way, part).start()
+    for way in (1, -1):
+        w_own(way, 0 if way > 0 else 1).start()
+        tok_own(way, 0 if way > 0 else 1).start()
+    for way in (1, -1):
+        tok_own(way, 1 if way > 0 else 0).start()
 
     def step_body(step, carry):
+        @pl.when((step >= LAG_RELAY) & (step < UNITS + LAG_RELAY))
+        def _():
+            done = step - LAG_RELAY
+            for part in (0, 1):
+                to = (y + (1 if part == 0 else 3)) % 4
+                relay_copy(done, part).wait_recv()
+                added = parts[done, to, part].astype(F32) + relay[done, part].astype(F32)
+                parts[done, to, part] = added.astype(BF)
+
+        @pl.when((step >= LAG_RELAY) & (step < UNITS + LAG_RELAY))
+        def _():
+            for part in (0, 1):
+                sum_copy(step - LAG_RELAY, part).start()
+
+        @pl.when(step >= LAG_SUM)
+        def _():
+            done = step - LAG_SUM
+            rows, columns = unit_of(done)
+            for part in (0, 1):
+                sum_copy(done, part).wait_recv()
+            total = parts[done, y].astype(F32) + arrived[done, 0].astype(F32)
+            total = (total + arrived[done, 1].astype(F32)).astype(BF)
+
+            @pl.when(rows == 0)
+            def _():
+                for part in (0, 1):
+                    final[z, (x + places_on(columns, part)) % 4, part] = total[part]
+
+            @pl.when(rows > 0)
+            def _():
+                sums[done] = total
+                for part in (0, 1):
+                    final_copy(done, part).start()
+
         @pl.when(step == 1)
         def _():
             loads[3].wait()
@@ -288,59 +323,63 @@
                     chosen_down, toks[0, block], LAST, preferred_element_type=F32
                 )
             for n in (1, 2, 3):
+                shrink_copy(n).start()
+            for n in (1, 2, 3):
                 index_x_arrival(n).wait_recv()
             for n in (1, 2, 3):
                 index_z(n).start()
-                shrink_copy(n).start()
+
+        @pl.when(step == 1)
+        def _():
+            loads[4].wait()
+            for way in (1, -1):
+                part = 0 if way > 0 else 1
+                w_own(way, part).wait_send()
+                up_near(way % 4).start()
+                up_cross(part).start()
             for part in (0, 1):
                 tok_arrival(1, part).wait_recv()
                 tok_partner(1, part).start()
             for part in (0, 1):
+                w_arrival(1, part).wait_recv()
+
+        @pl.when(step == 2)
+        def _():
+            for way in (1, -1):
+                part = 0 if way > 0 else 1
+                up_near(way % 4).wait_send()
+                up_cross(part).wait_send()
+                w_own(way, 1 - part).start()
+            for part in (0, 1):
                 tok_partner_arrival(1, part).wait_recv()
 
-        @pl.when(step == 2)
-        def _():
-            for part in (0, 1):
-                w_arrival(1, part).wait_recv()
+        @pl.when(step == 3)
+        def _():
+            for way in (1, -1):
+                part = 0 if way > 0 else 1
+                tok_own(way, 1 - part).wait_send()
+                tok_forward(part).start()
 
         @pl.when(step == 4)
         def _():
             for part in (0, 1):
-                tok_arrival(2, part).wait_recv()
-                tok_forward(part).start()
-                tok_partner(2, part).start()
-            loads[4].wait()
+                tok_partner_arrival(2, part).wait_recv()
+
+        @pl.when(step == 6)
+        def _():
             for part in (0, 1):
                 w_arrival(2, part).wait_recv()
-            for part in (0, 1):
-                up_near(1 + 2 * part).start()
-                up_cross(part).start()
-
-        @pl.when(step == 5)
-        def _():
-            for part in (0, 1):
-                tok_partner_arrival(2, part).wait_recv()
-
-        @pl.when(step == 6)
-        def _():
-            for part in (0, 1):
-                up_cross(part).wait_recv()
-                up_relay(part).start()
-            for part in (0, 1):
                 w_forward(part).start()
-
-        @pl.when(step == 7)
-        def _():
             for part in (0, 1):
                 tok_arrival(3, part).wait_recv()
                 tok_partner(3, part).start()
 
-        @pl.when(step == 8)
+        @pl.when(step == 7)
         def _():
             for part in (0, 1):
                 tok_partner_arrival(3, part).wait_recv()
 
-        @pl.when(step == 11)
+        @pl.when(step == 10)
         def _():
             for part in (0, 1):
                 w_arrival(3, part).wait_recv()
@@ -356,44 +395,19 @@
                 tile = result[:, block * BLOCK : (block + 1) * BLOCK]
                 parts[step, block] = tile.reshape(2, HALF, BLOCK)
 
-        @pl.when((step >= LAG_RELAY) & (step < UNITS + LAG_RELAY))
-        def _():
-            done = step - LAG_RELAY
-            for part in (0, 1):
-                to = (y + (1 if part == 0 else 3)) % 4
-                relay_copy(done, part).wait_recv()
-                added = parts[done, to, part].astype(F32) + relay[done, part].astype(F32)
-                parts[done, to, part] = added.astype(BF)
-
         @pl.when(step < UNITS)
         def _():
             for part in (0, 1):
                 relay_copy(step, part).start()
 
-        @pl.when((step >= LAG_RELAY) & (step < UNITS + LAG_RELAY))
-        def _():
-            for part in (0, 1):
-                sum_copy(step - LAG_RELAY, part).start()
-
-        @pl.when(step >= LAG_SUM)
-        def _():
-            done = step - LAG_SUM
-            rows, columns = unit_of(done)
-            for part in (0, 1):
-                sum_copy(done, part).wait_recv()
-            total = parts[done, y].astype(F32) + arrived[done, 0].astype(F32)
-            total = (total + arrived[done, 1].astype(F32)).astype(BF)
-
-            @pl.when(rows == 0)
-            def _():
-                for part in (0, 1):
-                    final[z, (x + places_on(columns, part)) % 4, part] = total[part]
-
-            @pl.when(rows > 0)
-            def _():
-                sums[done] = total
-                for part in (0, 1):
-                    final_copy(done, part).start()
+        @pl.when(step == 3)
+        def _():
+            for part in (0, 1):
+                tok_arrival(2, part).wait_recv()
+                tok_partner(2, part).start()
+            for part in (0, 1):
+                up_cross(part).wait_recv()
+                up_relay(part).start()
 
         @pl.when(step == PICK_STEP)
         def _():
@@ -451,13 +465,11 @@
         up_pair(1).wait_send()
         up_far().wait_send()
         for part in (0, 1):
-            for way in (1, -1):
-                w_own(way, part).wait_send()
-                tok_own(way, part).wait_send()
+            way = 1 if part == 0 else -1
+            w_own(way, 1 - part).wait_send()
+            tok_own(way, part).wait_send()
             w_forward(part).wait_send()
             tok_forward(part).wait_send()
-            up_near(1 + 2 * part).wait_send()
-            up_cross(part).wait_send()
             up_relay(part).wait_send()
             for kind in (1, 2, 3):
                 tok_partner(kind, part).wait_send()

time: 76 us -> 72.5 us (0.954)
  the two profiles are of different devices: /device:TPU:64 before, /device:TPU:8 now
where the time goes in v3:
time: 72.5 us; the launch traced here: 71.5 us
  Pallas kernels  69.1 us (95%)
  local copies, waits for them, and re-layouts  2.36 us (3%)
    pallas_call x1, Pallas kernels, body(): pl.pallas_call(kernel, out_shape=jax.ShapeDtypeStruct((BLOCK, 4 * SLICE),...  69.1 us
    unnamed x1, local copies, waits for them, and re-layouts  2.36 us

profile of v3, /device:TPU:8, one launch (start us, length us, event | category | flops | bytes accessed | tf_op | source)
XLA Modules:
  0.0 71.5 jit_solution(12273031186503509892)
XLA Ops:
  0.0 69.1 %shard_map.64 = bf16[128,4608]{1,0:T(8,128)(2,1)} custom-call(s32[4]{0:T(128)} %idx_hbm.1, s32[4]{0:T(128)} %live_hbm.1, bf16[4,128,1152]{2,1,0:T(8,128)(2,1)} %bitcast.4, bf16[2,144,1152]{2,1,0:T(8,128)(2,1)} %bitcast.5, bf16[64,16,1152]{2,1,0:T(8,128)(2,1)} %down_hbm.1, bf16[4,16,4608]{2,1,0:T(8,128)(2,1)} %up_hbm.1), custom_call_target="tpu_custom_call" | custom-call | tf_op jit(solution)/shard_map/pallas_call | solution.py:531
  69.2 2.4 %copy.8 = bf16[128,4608]{1,0:T(8,128)(2,1)} copy(bf16[128,4608]{1,0:T(8,128)(2,1)} %shard_map.64) | data formatting | bytes 2359296

commit v4 on v3

--- a/solution.py
+++ b/solution.py
@@ -18,8 +18,9 @@
 LAG_RELAY = 2
 LAG_SUM = 4
 PICK_STEP = 6
-PAIR_STEP = 8
-FAR_STEP = 12
+PAIR_STEP = 9
+FAR_STEP = 15
+AWAY = (2, 12)
 BF = jnp.bfloat16
 F32 = jnp.float32
 LAST = (((1,), (1,)), ((), ()))
@@ -48,12 +49,10 @@
 
 
 def kernel(
-    idx_hbm, live_hbm, tok_hbm, wt_hbm, down_hbm, up_hbm, out_hbm,
-    toks, wts, down, up, parts, relay, arrived, sums, final, upfin, out,
+    idx_hbm, live_hbm, tok_hbm, wt_hbm, down_hbm, up_hbm, out_ref,
+    toks, wts, down, up, parts, relay, arrived, sums, final, upfin,
     idx_ref, live_ref, idx_all, idx_s, spread, transit, picked, zpicks, chosen, shr, shr_in,
-    local_sem, out_sem, tok_s, tok_r, tokp_s, tokp_r, w_s, w_r,
-    r1_s, r1_r, r2_s, r2_r, fin_s, fin_r,
-    ixa_s, ixa_r, ixb_s, ixb_r, u1_s, u1_r, u2_s, u2_r, u3_s, u3_r, sh_s, sh_r,
+    local_sem, one, tok_s, tok_r, tokp_r, w_s, w_r, r1_r, r2_r, fin_r, u2_r,
 ):
     gx = lax.axis_index("gx")
     y = lax.axis_index("gy")
@@ -100,11 +99,10 @@
             tok_s.at[2, part], tok_r.at[2, part], on_ring(1 if part == 0 else -1),
         )
 
-    def tok_partner(kind, part, sent=True):
-        block = 2 * (core if sent else 1 - core) + part
-        return remote(
-            toks.at[kind, block], toks.at[kind, block],
-            tokp_s.at[kind - 1, part], tokp_r.at[kind - 1, part], partner,
+    def tok_partner(kind, part):
+        block = 2 * core + part
+        return remote(
+            toks.at[kind, block], toks.at[kind, block], one.at[0], tokp_r.at[kind - 1], partner
         )
 
     def tok_arrival(kind, part):
@@ -114,8 +112,11 @@
             tok_s.at[kind - 1, part], tok_r.at[kind - 1, part], partner,
         )
 
-    def tok_partner_arrival(kind, part):
-        return tok_partner(kind, part, False)
+    def tok_partner_arrival(kind):
+        blocks = pl.ds(2 * (1 - core), 2)
+        return remote(
+            toks.at[kind, blocks], toks.at[kind, blocks], one.at[0], tokp_r.at[kind - 1], partner
+        )
 
     def w_own(way, part):
         kind = kind_of(way, part)
@@ -139,14 +140,14 @@
     def relay_copy(step, part):
         return remote(
             parts.at[step, (y + 2) % 4, part], relay.at[step, part],
-            r1_s.at[step, part], r1_r.at[step, part], along_y(1 if part == 0 else 3),
+            one.at[1], r1_r.at[step % 4, part], along_y(1 if part == 0 else 3),
         )
 
     def sum_copy(step, part):
         way = 1 if part == 0 else 3
         return remote(
             parts.at[step, (y + way) % 4], arrived.at[step, part],
-            r2_s.at[step, part], r2_r.at[step, part], along_y(way),
+            one.at[2], r2_r.at[step % 4, part], along_y(way),
         )
 
     def final_copy(step, part):
@@ -154,58 +155,35 @@
         chunk = (x + places_on(columns, part)) % 4
         return remote(
             sums.at[step, part], final.at[z, chunk, part],
-            fin_s.at[step, part], fin_r.at[z, chunk, part], along_z(places_on(rows, y % 2)),
-        )
-
-    def final_arrival(place, chunk, part):
-        return remote(
-            final.at[place, chunk, part], final.at[place, chunk, part],
-            fin_s.at[0, part], fin_r.at[place, chunk, part], along_z(1),
-        )
+            one.at[3], fin_r.at[z], along_z(places_on(rows, y % 2)),
+        )
+
+    def final_arrival(place):
+        return remote(final.at[place], final.at[place], one.at[3], fin_r.at[place], along_z(1))
 
     def index_x(step):
-        return remote(
-            idx_all.at[z, x], idx_all.at[z, x], ixa_s.at[step - 1], ixa_r.at[step - 1], along_x(step)
-        )
-
-    def index_x_arrival(step):
-        place = (x + 4 - step) % 4
-        return remote(
-            idx_all.at[z, place], idx_all.at[z, place],
-            ixa_s.at[step - 1], ixa_r.at[step - 1], along_x(step),
-        )
+        return remote(idx_all.at[z, x], idx_all.at[z, x], one.at[4], one.at[5], along_x(step))
 
     def index_z(step):
-        return remote(
-            idx_all.at[z], idx_all.at[z], ixb_s.at[step - 1], ixb_r.at[step - 1], along_z(step)
-        )
-
-    def index_z_arrival(step):
-        place = (z + 4 - step) % 4
-        return remote(
-            idx_all.at[place], idx_all.at[place],
-            ixb_s.at[step - 1], ixb_r.at[step - 1], along_z(step),
-        )
+        return remote(idx_all.at[z], idx_all.at[z], one.at[6], one.at[7], along_z(step))
+
+    index_x_three = remote(
+        idx_all.at[0, pl.ds(0, 3)], idx_all.at[0, pl.ds(0, 3)], one.at[4], one.at[5], along_x(1)
+    )
+    index_z_three = remote(
+        idx_all.at[pl.ds(0, 3)], idx_all.at[pl.ds(0, 3)], one.at[6], one.at[7], along_z(1)
+    )
 
     def up_columns(step):
         return pl.ds(pl.multiple_of((x + step) % 4 * SLICE, SLICE), SLICE)
 
     def up_near(step):
-        which = step // 2
-        return remote(
-            up.at[:, :, up_columns(step)], spread.at[x], u1_s.at[which], u1_r.at[which], along_x(step)
-        )
-
-    def up_near_arrival(step):
-        which, place = step // 2, (x + 4 - step) % 4
-        return remote(
-            spread.at[place], spread.at[place], u1_s.at[which], u1_r.at[which], along_x(step)
-        )
+        return remote(up.at[:, :, up_columns(step)], spread.at[x], one.at[8], one.at[9], along_x(step))
 
     def up_cross(part):
         return remote(
             up.at[pl.ds(2 * part, 2), :, up_columns(2)], transit.at[part],
-            u1_s.at[2 + part], u1_r.at[2 + part], along_x(1 if part == 0 else 3),
+            one.at[8], one.at[10], along_x(1 if part == 0 else 3),
         )
 
     def up_relay(part):
@@ -213,8 +191,11 @@
         place = (x + 4 - step) % 4
         return remote(
             transit.at[part], spread.at[place, pl.ds(2 * part, 2)],
-            u1_s.at[4 + part], u1_r.at[4 + part], along_x(step),
-        )
+            one.at[11], one.at[9], along_x(step),
+        )
+
+    up_three = remote(spread.at[pl.ds(0, 3)], spread.at[pl.ds(0, 3)], one.at[8], one.at[9], along_x(1))
+    up_transit = remote(transit, transit, one.at[11], one.at[10], along_x(1))
 
     mate = 1 - 2 * (z % 2)
     far = 3 - 2 * z
@@ -222,28 +203,26 @@
     def up_pair(part):
         chunk = z + mate if part == 0 else 3 - (z + mate)
         return remote(
-            picked.at[chunk], zpicks.at[part], u2_s.at[part], u2_r.at[part], along_z(mate + 4)
+            picked.at[chunk], zpicks.at[part], one.at[12], u2_r.at[part], along_z(mate + 4)
         )
 
     def up_far():
-        return remote(picked.at[3 - z], zpicks.at[2], u2_s.at[2], u2_r.at[2], along_z(far + 4))
+        return remote(picked.at[3 - z], zpicks.at[2], one.at[12], u2_r.at[2], along_z(far + 4))
 
     def up_last(step):
         return remote(
-            chosen.at[(x + step) % 4], upfin.at[x], u3_s.at[step - 1], u3_r.at[step - 1], along_x(step)
-        )
-
-    def up_last_arrival(step):
-        place = (x + 4 - step) % 4
-        return remote(
-            upfin.at[place], upfin.at[place], u3_s.at[step - 1], u3_r.at[step - 1], along_x(step)
+            chosen.at[(x + step) % 4], upfin.at[x], one.at[13], one.at[14], along_x(step)
         )
 
     def shrink_copy(step):
         return remote(
-            shr.at[(y + step) % 4], shr_in.at[step - 1],
-            sh_s.at[step - 1], sh_r.at[step - 1], along_y(step),
-        )
+            shr.at[(y + step) % 4], shr_in.at[step - 1], one.at[15], one.at[16], along_y(step)
+        )
+
+    up_last_three = remote(
+        chosen.at[pl.ds(0, 3)], upfin.at[pl.ds(0, 3)], one.at[13], one.at[14], along_x(1)
+    )
+    shrink_three = remote(shr_in, shr_in, one.at[15], one.at[16], along_y(1))
 
     loads = [
         pltpu.make_async_copy(idx_hbm, idx_ref, local_sem.at[4]),
@@ -279,6 +258,9 @@
     for way in (1, -1):
         tok_own(way, 1 if way > 0 else 0).start()
 
+    to_scalars = pltpu.make_async_copy(idx_all, idx_s, local_sem.at[0])
+    own_columns = pltpu.make_async_copy(up.at[:, :, up_columns(0)], spread.at[x], local_sem.at[1])
+
     def step_body(step, carry):
         @pl.when((step >= LAG_RELAY) & (step < UNITS + LAG_RELAY))
         def _():
@@ -324,8 +306,7 @@
                 )
             for n in (1, 2, 3):
                 shrink_copy(n).start()
-            for n in (1, 2, 3):
-                index_x_arrival(n).wait_recv()
+            index_x_three.wait_recv()
             for n in (1, 2, 3):
                 index_z(n).start()
 
@@ -345,13 +326,11 @@
 
         @pl.when(step == 2)
         def _():
+            up_three.wait_send()
             for way in (1, -1):
                 part = 0 if way > 0 else 1
-                up_near(way % 4).wait_send()
-                up_cross(part).wait_send()
                 w_own(way, 1 - part).start()
-            for part in (0, 1):
-                tok_partner_arrival(1, part).wait_recv()
+            tok_partner_arrival(1).wait_recv()
 
         @pl.when(step == 3)
         def _():
@@ -362,8 +341,7 @@
 
         @pl.when(step == 4)
         def _():
-            for part in (0, 1):
-                tok_partner_arrival(2, part).wait_recv()
+            tok_partner_arrival(2).wait_recv()
 
         @pl.when(step == 6)
         def _():
@@ -376,8 +354,7 @@
 
         @pl.when(step == 7)
         def _():
-            for part in (0, 1):
-                tok_partner_arrival(3, part).wait_recv()
+            tok_partner_arrival(3).wait_recv()
 
         @pl.when(step == 10)
         def _():
@@ -405,25 +382,18 @@
             for part in (0, 1):
                 tok_arrival(2, part).wait_recv()
                 tok_partner(2, part).start()
-            for part in (0, 1):
-                up_cross(part).wait_recv()
+            up_transit.wait_recv()
+            for part in (0, 1):
                 up_relay(part).start()
+            own_columns.start()
 
         @pl.when(step == PICK_STEP)
         def _():
-            for n in (1, 2, 3):
-                index_z_arrival(n).wait_recv()
-            to_scalars = pltpu.make_async_copy(idx_all, idx_s, local_sem.at[0])
+            index_z_three.wait_recv()
             to_scalars.start()
-            own = pltpu.make_async_copy(
-                up.at[:, :, pl.ds(pl.multiple_of(x * SLICE, SLICE), SLICE)], spread.at[x], local_sem.at[1]
-            )
-            own.start()
-            for part in (0, 1):
-                up_near_arrival(1 + 2 * part).wait_recv()
-                up_relay(part).wait_recv()
+            up_three.wait_recv()
             to_scalars.wait()
-            own.wait()
+            own_columns.wait()
             for to_z in range(4):
                 for to_x in range(4):
                     local = idx_s[to_z, to_x, 0, y] - 16 * z
@@ -456,39 +426,24 @@
     lax.fori_loop(0, UNITS + LAG_SUM, step_body, 0)
 
     def finish_sends():
-        for n in (1, 2, 3):
-            index_x(n).wait_send()
-            index_z(n).wait_send()
-            up_last(n).wait_send()
-            shrink_copy(n).wait_send()
-        up_pair(0).wait_send()
-        up_pair(1).wait_send()
-        up_far().wait_send()
+        index_x_three.wait_send()
+        index_z_three.wait_send()
+        shrink_three.wait_send()
+        up_transit.wait_send()
+        remote(zpicks, zpicks, one.at[12], u2_r.at[0], partner).wait_send()
+        up_last_three.wait_send()
         for part in (0, 1):
             way = 1 if part == 0 else -1
             w_own(way, 1 - part).wait_send()
             tok_own(way, part).wait_send()
             w_forward(part).wait_send()
             tok_forward(part).wait_send()
-            up_relay(part).wait_send()
-            for kind in (1, 2, 3):
-                tok_partner(kind, part).wait_send()
-
-        def drain(step, carry):
-            for part in (0, 1):
-                relay_copy(step, part).wait_send()
-                sum_copy(step, part).wait_send()
-
-                @pl.when(unit_of(step)[0] > 0)
-                def _():
-                    final_copy(step, part).wait_send()
-
-            return carry
-
-        lax.fori_loop(0, UNITS, drain, 0)
-
-    for n in (1, 2, 3):
-        shrink_copy(n).wait_recv()
+        passed = toks.at[pl.ds(1, 3), pl.ds(0, 2)]
+        remote(passed, passed, one.at[0], tokp_r.at[0], partner).wait_send()
+        remote(relay, relay, one.at[1], r1_r.at[0, 0], partner).wait_send()
+        remote(arrived, arrived, one.at[2], r2_r.at[0, 0], partner).wait_send()
+
+    shrink_three.wait_recv()
     low = (shr[y] + shr_in[0] + (shr_in[1] + shr_in[2])).astype(BF)
     same = lax.broadcasted_iota(jnp.int32, (BLOCK, BLOCK), 0) == lax.broadcasted_iota(
         jnp.int32, (BLOCK, BLOCK), 1
@@ -498,30 +453,22 @@
     doubled = (2.0 * turned).astype(BF)
     loads[5].wait()
     live = lax.broadcasted_iota(jnp.int32, (BLOCK, 1), 0) < live_ref[y]
-    for n in (1, 2, 3):
-        up_last_arrival(n).wait_recv()
-
-    def write_out(n):
-        place = (z + n) % 4
-        columns = pl.ds(pl.multiple_of(place * SLICE, SLICE), SLICE)
-        return pltpu.make_async_copy(out.at[n], out_hbm.at[:, columns], out_sem.at[n])
+    up_last_three.wait_recv()
 
     for n in (0, 1, 3, 2):
         place = (z + n) % 4
         if n:
-            for chunk in range(4):
-                for part in (0, 1):
-                    final_arrival(place, chunk, part).wait_recv()
+            final_arrival(place).wait_recv()
         base = lax.dot_general(
             eye, final[place].reshape(SLICE, BLOCK), LAST, preferred_element_type=F32
         )
         extra = jnp.dot(doubled, upfin[place], preferred_element_type=F32)
-        out[n] = jnp.where(live, base + extra, 0.0).astype(BF)
-        write_out(n).start()
+        columns = pl.ds(pl.multiple_of(place * SLICE, SLICE), SLICE)
+        out_ref[:, columns] = jnp.where(live, base + extra, 0.0).astype(BF)
         if n == 0:
             finish_sends()
-    for n in range(4):
-        write_out(n).wait()
+    gone = sums.at[pl.ds(*AWAY)]
+    remote(gone, gone, one.at[3], fin_r.at[z], partner).wait_send()
 
 
 def body(tokens, base_up_weight, adapter_down_weight, adapter_up_weight, block_adapter_index, request_rows):
@@ -530,9 +477,9 @@
     any_space = pl.BlockSpec(memory_space=pl.ANY)
     return pl.pallas_call(
         kernel,
-        out_shape=jax.ShapeDtypeStruct((BLOCK, 4 * SLICE), BF),
+        out_shape=pltpu.VMEM((BLOCK, 4 * SLICE), BF),
         in_specs=[any_space] * 6,
-        out_specs=any_space,
+        out_specs=pl.BlockSpec(memory_space=pltpu.VMEM),
         scratch_shapes=[
             pltpu.VMEM((4, 4, BLOCK, WIDTH), BF),
             pltpu.VMEM((4, 2, HALF, WIDTH), BF),
@@ -544,7 +491,6 @@
             pltpu.VMEM((UNITS, *half_tile), BF),
             pltpu.VMEM((4, 4, *half_tile), BF),
             pltpu.VMEM((4, RANK, SLICE), BF),
-            pltpu.VMEM((4, BLOCK, SLICE), BF),
             pltpu.SMEM((4,), jnp.int32),
             pltpu.SMEM((4,), jnp.int32),
             pltpu.VMEM((4, 4, 1, 128), jnp.int32),
@@ -556,16 +502,12 @@
             pltpu.VMEM((4, RANK, SLICE), BF),
             pltpu.VMEM((4, RANK, BLOCK), F32),
             pltpu.VMEM((3, RANK, BLOCK), F32),
-            dma((6,)), dma((4,)),
-            dma((3, 2)), dma((3, 2)), dma((3, 2)), dma((3, 2)), dma((3, 2)), dma((3, 2)),
-            dma((UNITS, 2)), dma((UNITS, 2)), dma((UNITS, 2)), dma((UNITS, 2)),
-            dma((UNITS, 2)), dma((4, 4, 2)),
-            dma((3,)), dma((3,)), dma((3,)), dma((3,)),
-            dma((6,)), dma((6,)), dma((3,)), dma((3,)), dma((3,)), dma((3,)),
-            dma((3,)), dma((3,)),
+            dma((6,)), dma((17,)),
+            dma((3, 2)), dma((3, 2)), dma((3,)), dma((3, 2)), dma((3, 2)),
+            dma((4, 2)), dma((4, 2)), dma((4,)), dma((3,)),
         ],
         compiler_params=pltpu.CompilerParams(
-            collective_id=0, has_side_effects=True, vmem_limit_bytes=67043328
+            collective_id=0, has_side_effects=True, vmem_limit_bytes=60000000
         ),
     )(
         block_adapter_index,

time: 72.5 us -> 68.5 us (0.945)
  the two profiles are of different devices: /device:TPU:8 before, /device:TPU:1 now
where the time goes in v4:
time: 68.5 us; the launch traced here: 68.4 us
  Pallas kernels  67.4 us (98%)
  local copies, waits for them, and re-layouts  1.02 us (1%)
    pallas_call x1, Pallas kernels, body(): pl.pallas_call(kernel, out_shape=pltpu.VMEM((BLOCK, 4 * SLICE), BF), in_s...  67.4 us

profile of v4, /device:TPU:1, one launch (start us, length us, event | category | flops | bytes accessed | tf_op | source)
XLA Modules:
  0.0 68.4 jit_solution(4042602787675027877)
XLA Ops:
  0.0 67.4 %shard_map.64 = bf16[128,4608]{1,0:T(8,128)(2,1)S(1)} custom-call(s32[4]{0:T(128)} %idx_hbm.1, s32[4]{0:T(128)} %live_hbm.1, bf16[4,128,1152]{2,1,0:T(8,128)(2,1)} %bitcast.4, bf16[2,144,1152]{2,1,0:T(8,128)(2,1)} %bitcast.5, bf16[64,16,1152]{2,1,0:T(8,128)(2,1)} %down_hbm.1, bf16[4,16,4608]{2,1,0:T(8,128)(2,1)} %up_hbm.1), custom_call_target="tpu_custom_call" | custom-call | tf_op jit(solution)/shard_map/pallas_call | solution.py:478
  67.4 1.0 %copy.8 = bf16[128,4608]{1,0:T(8,128)(2,1)} copy(bf16[128,4608]{1,0:T(8,128)(2,1)S(1)} %shard_map.64) | data formatting | bytes 2359296

commit v5 on v4

--- a/solution.py
+++ b/solution.py
@@ -17,9 +17,9 @@
 UNITS = 16
 LAG_RELAY = 2
 LAG_SUM = 4
-PICK_STEP = 6
-PAIR_STEP = 9
-FAR_STEP = 15
+PICK_STEP = 5
+PAIR_STEP = 7
+FAR_STEP = 18
 AWAY = (2, 12)
 BF = jnp.bfloat16
 F32 = jnp.float32
@@ -27,8 +27,8 @@
 
 
 ORDER = (
-    (0, 0), (0, 1), (1, 0), (1, 1), (2, 0), (2, 1), (1, 2), (3, 0),
-    (2, 2), (3, 1), (1, 3), (3, 2), (2, 3), (3, 3), (0, 2), (0, 3),
+    (0, 0), (0, 1), (1, 0), (1, 1), (3, 0), (3, 1), (1, 2), (3, 2),
+    (2, 0), (2, 1), (3, 3), (1, 3), (2, 2), (2, 3), (0, 2), (0, 3),
 )
 
 
@@ -89,14 +89,14 @@
         kind, block = kind_of(way, part), 2 * core + part
         return remote(
             toks.at[0, block], toks.at[kind, block],
-            tok_s.at[kind - 1, part], tok_r.at[kind - 1, part], on_ring(way),
+            tok_s.at[kind - 1], tok_r.at[kind - 1], on_ring(way),
         )
 
     def tok_forward(part):
         block = 2 * core + part
         return remote(
             toks.at[1, block], toks.at[3, block],
-            tok_s.at[2, part], tok_r.at[2, part], on_ring(1 if part == 0 else -1),
+            tok_s.at[2], tok_r.at[2], on_ring(1 if part == 0 else -1),
         )
 
     def tok_partner(kind, part):
@@ -105,11 +105,10 @@
             toks.at[kind, block], toks.at[kind, block], one.at[0], tokp_r.at[kind - 1], partner
         )
 
-    def tok_arrival(kind, part):
-        block = 2 * core + part
-        return remote(
-            toks.at[kind, block], toks.at[kind, block],
-            tok_s.at[kind - 1, part], tok_r.at[kind - 1, part], partner,
+    def tok_pair(kind):
+        blocks = pl.ds(2 * core, 2)
+        return remote(
+            toks.at[kind, blocks], toks.at[kind, blocks], tok_s.at[kind - 1], tok_r.at[kind - 1], partner
         )
 
     def tok_partner_arrival(kind):
@@ -122,20 +121,17 @@
         kind = kind_of(way, part)
         return remote(
             wts.at[0, part], wts.at[kind, part],
-            w_s.at[kind - 1, part], w_r.at[kind - 1, part], along_x(way % 4),
+            w_s.at[kind - 1], w_r.at[kind - 1], along_x(way % 4),
         )
 
     def w_forward(part):
         return remote(
             wts.at[1, part], wts.at[3, part],
-            w_s.at[2, part], w_r.at[2, part], along_x(1 if part == 0 else 3),
-        )
-
-    def w_arrival(kind, part):
-        return remote(
-            wts.at[kind, part], wts.at[kind, part],
-            w_s.at[kind - 1, part], w_r.at[kind - 1, part], along_x(1),
-        )
+            w_s.at[2], w_r.at[2], along_x(1 if part == 0 else 3),
+        )
+
+    def w_pair(kind):
+        return remote(wts.at[kind], wts.at[kind], w_s.at[kind - 1], w_r.at[kind - 1], along_x(1))
 
     def relay_copy(step, part):
         return remote(
@@ -250,32 +246,17 @@
     loads[2].wait()
     pl.semaphore_wait(barrier, len(peers))
 
+    for way in (1, -1):
+        tok_own(way, 0 if way > 0 else 1).start()
     for n in (1, 2, 3):
         index_x(n).start()
     for way in (1, -1):
         w_own(way, 0 if way > 0 else 1).start()
-        tok_own(way, 0 if way > 0 else 1).start()
-    for way in (1, -1):
-        tok_own(way, 1 if way > 0 else 0).start()
 
     to_scalars = pltpu.make_async_copy(idx_all, idx_s, local_sem.at[0])
     own_columns = pltpu.make_async_copy(up.at[:, :, up_columns(0)], spread.at[x], local_sem.at[1])
 
     def step_body(step, carry):
-        @pl.when((step >= LAG_RELAY) & (step < UNITS + LAG_RELAY))
-        def _():
-            done = step - LAG_RELAY
-            for part in (0, 1):
-                to = (y + (1 if part == 0 else 3)) % 4
-                relay_copy(done, part).wait_recv()
-                added = parts[done, to, part].astype(F32) + relay[done, part].astype(F32)
-                parts[done, to, part] = added.astype(BF)
-
-        @pl.when((step >= LAG_RELAY) & (step < UNITS + LAG_RELAY))
-        def _():
-            for part in (0, 1):
-                sum_copy(step - LAG_RELAY, part).start()
-
         @pl.when(step >= LAG_SUM)
         def _():
             done = step - LAG_SUM
@@ -295,6 +276,20 @@
                 sums[done] = total
                 for part in (0, 1):
                     final_copy(done, part).start()
+
+        @pl.when((step >= LAG_RELAY) & (step < UNITS + LAG_RELAY))
+        def _():
+            done = step - LAG_RELAY
+            for part in (0, 1):
+                to = (y + (1 if part == 0 else 3)) % 4
+                relay_copy(done, part).wait_recv()
+                added = parts[done, to, part].astype(F32) + relay[done, part].astype(F32)
+                parts[done, to, part] = added.astype(BF)
+
+        @pl.when((step >= LAG_RELAY) & (step < UNITS + LAG_RELAY))
+        def _():
+            for part in (0, 1):
+                sum_copy(step - LAG_RELAY, part).start()
 
         @pl.when(step == 1)
         def _():
@@ -313,16 +308,16 @@
         @pl.when(step == 1)
         def _():
             loads[4].wait()
+            w_pair(1).wait_send()
             for way in (1, -1):
                 part = 0 if way > 0 else 1
-                w_own(way, part).wait_send()
                 up_near(way % 4).start()
                 up_cross(part).start()
-            for part in (0, 1):
-                tok_arrival(1, part).wait_recv()
+            tok_pair(1).wait_recv()
+            for part in (0, 1):
+                tok_forward(part).start()
                 tok_partner(1, part).start()
-            for part in (0, 1):
-                w_arrival(1, part).wait_recv()
+            w_pair(1).wait_recv()
 
         @pl.when(step == 2)
         def _():
@@ -334,32 +329,30 @@
 
         @pl.when(step == 3)
         def _():
+            tok_pair(3).wait_send()
             for way in (1, -1):
-                part = 0 if way > 0 else 1
-                tok_own(way, 1 - part).wait_send()
-                tok_forward(part).start()
+                tok_own(way, 1 if way > 0 else 0).start()
 
         @pl.when(step == 4)
         def _():
+            tok_partner_arrival(3).wait_recv()
+
+        @pl.when(step == 6)
+        def _():
+            w_pair(2).wait_recv()
+            for part in (0, 1):
+                w_forward(part).start()
+            tok_pair(2).wait_recv()
+            for part in (0, 1):
+                tok_partner(2, part).start()
+
+        @pl.when(step == 8)
+        def _():
             tok_partner_arrival(2).wait_recv()
 
-        @pl.when(step == 6)
-        def _():
-            for part in (0, 1):
-                w_arrival(2, part).wait_recv()
-                w_forward(part).start()
-            for part in (0, 1):
-                tok_arrival(3, part).wait_recv()
-                tok_partner(3, part).start()
-
-        @pl.when(step == 7)
-        def _():
-            tok_partner_arrival(3).wait_recv()
-
         @pl.when(step == 10)
         def _():
-            for part in (0, 1):
-                w_arrival(3, part).wait_recv()
+            w_pair(3).wait_recv()
 
         @pl.when(step < UNITS)
         def _():
@@ -379,18 +372,21 @@
 
         @pl.when(step == 3)
         def _():
-            for part in (0, 1):
-                tok_arrival(2, part).wait_recv()
-                tok_partner(2, part).start()
+            tok_pair(3).wait_recv()
+            for part in (0, 1):
+                tok_partner(3, part).start()
             up_transit.wait_recv()
             for part in (0, 1):
                 up_relay(part).start()
             own_columns.start()
 
-        @pl.when(step == PICK_STEP)
+        @pl.when(step == PICK_STEP - 1)
         def _():
             index_z_three.wait_recv()
             to_scalars.start()
+
+        @pl.when(step == PICK_STEP)
+        def _():
             up_three.wait_recv()
             to_scalars.wait()
             own_columns.wait()
@@ -432,12 +428,10 @@
         up_transit.wait_send()
         remote(zpicks, zpicks, one.at[12], u2_r.at[0], partner).wait_send()
         up_last_three.wait_send()
-        for part in (0, 1):
-            way = 1 if part == 0 else -1
-            w_own(way, 1 - part).wait_send()
-            tok_own(way, part).wait_send()
-            w_forward(part).wait_send()
-            tok_forward(part).wait_send()
+        tok_pair(1).wait_send()
+        tok_pair(2).wait_send()
+        w_pair(2).wait_send()
+        w_pair(3).wait_send()
         passed = toks.at[pl.ds(1, 3), pl.ds(0, 2)]
         remote(passed, passed, one.at[0], tokp_r.at[0], partner).wait_send()
         remote(relay, relay, one.at[1], r1_r.at[0, 0], partner).wait_send()
@@ -503,7 +497,7 @@
             pltpu.VMEM((4, RANK, BLOCK), F32),
             pltpu.VMEM((3, RANK, BLOCK), F32),
             dma((6,)), dma((17,)),
-            dma((3, 2)), dma((3, 2)), dma((3,)), dma((3, 2)), dma((3, 2)),
+            dma((3,)), dma((3,)), dma((3,)), dma((3,)), dma((3,)),
             dma((4, 2)), dma((4, 2)), dma((4,)), dma((3,)),
         ],
         compiler_params=pltpu.CompilerParams(

time: 68.5 us -> 67.5 us (0.985)
  the two profiles are of different devices: /device:TPU:1 before, /device:TPU:8 now
where the time goes in v5:
time: 67.5 us; the launch traced here: 66.9 us
  Pallas kernels  65.9 us (98%)
  local copies, waits for them, and re-layouts  1.02 us (2%)
    pallas_call x1, Pallas kernels, body(): pl.pallas_call(kernel, out_shape=pltpu.VMEM((BLOCK, 4 * SLICE), BF), in_s...  65.9 us

profile of v5, /device:TPU:8, one launch (start us, length us, event | category | flops | bytes accessed | tf_op | source)
XLA Modules:
  0.0 66.9 jit_solution(12375375357700468094)
XLA Ops:
  0.0 65.9 %shard_map.64 = bf16[128,4608]{1,0:T(8,128)(2,1)S(1)} custom-call(s32[4]{0:T(128)} %idx_hbm.1, s32[4]{0:T(128)} %live_hbm.1, bf16[4,128,1152]{2,1,0:T(8,128)(2,1)} %bitcast.4, bf16[2,144,1152]{2,1,0:T(8,128)(2,1)} %bitcast.5, bf16[64,16,1152]{2,1,0:T(8,128)(2,1)} %down_hbm.1, bf16[4,16,4608]{2,1,0:T(8,128)(2,1)} %up_hbm.1), custom_call_target="tpu_custom_call" | custom-call | tf_op jit(solution)/shard_map/pallas_call | solution.py:472
  65.9 1.0 %copy.8 = bf16[128,4608]{1,0:T(8,128)(2,1)} copy(bf16[128,4608]{1,0:T(8,128)(2,1)S(1)} %shard_map.64) | data formatting | bytes 2359296

commit v6 on v5

--- a/solution.py
+++ b/solution.py
@@ -19,7 +19,7 @@
 LAG_SUM = 4
 PICK_STEP = 5
 PAIR_STEP = 7
-FAR_STEP = 18
+FAR_STEP = 16
 AWAY = (2, 12)
 BF = jnp.bfloat16
 F32 = jnp.float32

time: 67.5 us -> 67 us (level)
  Pallas kernels: 65.9 us -> 65.1 us
    pallas_call x1, Pallas kernels: 65.9 us -> 65.1 us  [body(): pl.pallas_call(kernel, out_shape=pltpu.VMEM((BLOCK, 4 * SLICE), BF), in_s...]
where the time goes in v6:
time: 67 us; the launch traced here: 66.1 us
  Pallas kernels  65.1 us (97%)
  local copies, waits for them, and re-layouts  1.02 us (2%)
    pallas_call x1, Pallas kernels, body(): pl.pallas_call(kernel, out_shape=pltpu.VMEM((BLOCK, 4 * SLICE), BF), in_s...  65.1 us

profile of v6, /device:TPU:8, one launch (start us, length us, event | category | flops | bytes accessed | tf_op | source)
XLA Modules:
  0.0 66.1 jit_solution(12605096206614360506)
XLA Ops:
  0.0 65.1 %shard_map.64 = bf16[128,4608]{1,0:T(8,128)(2,1)S(1)} custom-call(s32[4]{0:T(128)} %idx_hbm.1, s32[4]{0:T(128)} %live_hbm.1, bf16[4,128,1152]{2,1,0:T(8,128)(2,1)} %bitcast.4, bf16[2,144,1152]{2,1,0:T(8,128)(2,1)} %bitcast.5, bf16[64,16,1152]{2,1,0:T(8,128)(2,1)} %down_hbm.1, bf16[4,16,4608]{2,1,0:T(8,128)(2,1)} %up_hbm.1), custom_call_target="tpu_custom_call" | custom-call | tf_op jit(solution)/shard_map/pallas_call | solution.py:472
  65.1 1.0 %copy.8 = bf16[128,4608]{1,0:T(8,128)(2,1)} copy(bf16[128,4608]{1,0:T(8,128)(2,1)S(1)} %shard_map.64) | data formatting | bytes 2359296

commit v7 on v6

--- a/solution.py
+++ b/solution.py
@@ -449,7 +449,7 @@
     live = lax.broadcasted_iota(jnp.int32, (BLOCK, 1), 0) < live_ref[y]
     up_last_three.wait_recv()
 
-    for n in (0, 1, 3, 2):
+    for n in (0, 2, 1, 3):
         place = (z + n) % 4
         if n:
             final_arrival(place).wait_recv()

time: 67 us -> 66.8 us (level); the launches traced: 66.1 us -> 66.7 us
  no operation moved by 1% of the time
where the time goes in v7:
time: 66.8 us; the launch traced here: 66.7 us
  Pallas kernels  65.7 us (98%)
  local copies, waits for them, and re-layouts  1.02 us (2%)
    pallas_call x1, Pallas kernels, body(): pl.pallas_call(kernel, out_shape=pltpu.VMEM((BLOCK, 4 * SLICE), BF), in_s...  65.7 us

profile of v7, /device:TPU:8, one launch (start us, length us, event | category | flops | bytes accessed | tf_op | source)
XLA Modules:
  0.0 66.7 jit_solution(7210955083996860784)
XLA Ops:
  0.0 65.7 %shard_map.64 = bf16[128,4608]{1,0:T(8,128)(2,1)S(1)} custom-call(s32[4]{0:T(128)} %idx_hbm.1, s32[4]{0:T(128)} %live_hbm.1, bf16[4,128,1152]{2,1,0:T(8,128)(2,1)} %bitcast.4, bf16[2,144,1152]{2,1,0:T(8,128)(2,1)} %bitcast.5, bf16[64,16,1152]{2,1,0:T(8,128)(2,1)} %down_hbm.1, bf16[4,16,4608]{2,1,0:T(8,128)(2,1)} %up_hbm.1), custom_call_target="tpu_custom_call" | custom-call | tf_op jit(solution)/shard_map/pallas_call | solution.py:472
  65.7 1.0 %copy.8 = bf16[128,4608]{1,0:T(8,128)(2,1)} copy(bf16[128,4608]{1,0:T(8,128)(2,1)S(1)} %shard_map.64) | data formatting | bytes 2359296

commit v8 on v7

--- a/solution.py
+++ b/solution.py
@@ -111,6 +111,15 @@
             toks.at[kind, blocks], toks.at[kind, blocks], tok_s.at[kind - 1], tok_r.at[kind - 1], partner
         )
 
+    def tok_second(block):
+        return remote(
+            toks.at[0, block], toks.at[2, block],
+            tok_s.at[1], tok_r.at[1], on_ring(1 if block % 2 else -1),
+        )
+
+    tok_seconds = remote(toks.at[2], toks.at[2], tok_s.at[1], tok_r.at[1], partner)
+    tok_seconds_pass = remote(toks.at[2], toks.at[2], one.at[17], tokp_r.at[1], partner)
+
     def tok_partner_arrival(kind):
         blocks = pl.ds(2 * (1 - core), 2)
         return remote(
@@ -330,8 +339,12 @@
         @pl.when(step == 3)
         def _():
             tok_pair(3).wait_send()
-            for way in (1, -1):
-                tok_own(way, 1 if way > 0 else 0).start()
+
+            @pl.when(core == 1)
+            def _():
+                for block in range(4):
+                    tok_second(block).start()
+
 
         @pl.when(step == 4)
         def _():
@@ -342,13 +355,20 @@
             w_pair(2).wait_recv()
             for part in (0, 1):
                 w_forward(part).start()
-            tok_pair(2).wait_recv()
-            for part in (0, 1):
-                tok_partner(2, part).start()
+
+            @pl.when(core == 1)
+            def _():
+                tok_seconds.wait_recv()
+                tok_seconds_pass.start()
+
 
         @pl.when(step == 8)
         def _():
-            tok_partner_arrival(2).wait_recv()
+
+            @pl.when(core == 0)
+            def _():
+                tok_seconds_pass.wait_recv()
+
 
         @pl.when(step == 10)
         def _():
@@ -429,10 +449,15 @@
         remote(zpicks, zpicks, one.at[12], u2_r.at[0], partner).wait_send()
         up_last_three.wait_send()
         tok_pair(1).wait_send()
-        tok_pair(2).wait_send()
+
+        @pl.when(core == 1)
+        def _():
+            tok_seconds.wait_send()
+            tok_seconds_pass.wait_send()
+
         w_pair(2).wait_send()
         w_pair(3).wait_send()
-        passed = toks.at[pl.ds(1, 3), pl.ds(0, 2)]
+        passed = toks.at[pl.ds(1, 2), pl.ds(0, 2)]
         remote(passed, passed, one.at[0], tokp_r.at[0], partner).wait_send()
         remote(relay, relay, one.at[1], r1_r.at[0, 0], partner).wait_send()
         remote(arrived, arrived, one.at[2], r2_r.at[0, 0], partner).wait_send()
@@ -496,7 +521,7 @@
             pltpu.VMEM((4, RANK, SLICE), BF),
             pltpu.VMEM((4, RANK, BLOCK), F32),
             pltpu.VMEM((3, RANK, BLOCK), F32),
-            dma((6,)), dma((17,)),
+            dma((6,)), dma((18,)),
             dma((3,)), dma((3,)), dma((3,)), dma((3,)), dma((3,)),
             dma((4, 2)), dma((4, 2)), dma((4,)), dma((3,)),
         ],

time: 66.8 us -> 66.8 us (level)
  no operation moved by 1% of the time
where the time goes in v8:
time: 66.8 us; the launch traced here: 66.7 us
  Pallas kernels  65.7 us (98%)
  local copies, waits for them, and re-layouts  1.02 us (2%)
    pallas_call x1, Pallas kernels, body(): pl.pallas_call(kernel, out_shape=pltpu.VMEM((BLOCK, 4 * SLICE), BF), in_s...  65.7 us

profile of v8, /device:TPU:8, one launch (start us, length us, event | category | flops | bytes accessed | tf_op | source)
XLA Modules:
  0.0 66.7 jit_solution(11009060595527010573)
XLA Ops:
  0.0 65.7 %shard_map.64 = bf16[128,4608]{1,0:T(8,128)(2,1)S(1)} custom-call(s32[4]{0:T(128)} %idx_hbm.1, s32[4]{0:T(128)} %live_hbm.1, bf16[4,128,1152]{2,1,0:T(8,128)(2,1)} %bitcast.4, bf16[2,144,1152]{2,1,0:T(8,128)(2,1)} %bitcast.5, bf16[64,16,1152]{2,1,0:T(8,128)(2,1)} %down_hbm.1, bf16[4,16,4608]{2,1,0:T(8,128)(2,1)} %up_hbm.1), custom_call_target="tpu_custom_call" | custom-call | tf_op jit(solution)/shard_map/pallas_call | solution.py:497
  65.7 1.0 %copy.8 = bf16[128,4608]{1,0:T(8,128)(2,1)} copy(bf16[128,4608]{1,0:T(8,128)(2,1)S(1)} %shard_map.64) | data formatting | bytes 2359296
